TPU v7x, 768 devices: a whole 4x8x12 slice. The times are simulated.
768 devices in a mesh: gx: 32 (over y, z_lo), gy: 3 (over z_hi), gz: 8 (over x, core).
Axes of the slice: x: 4, y: 8, z: 12 (z_hi: 3, z_lo: 4; z = z_hi * 4 + z_lo), core: 2. Of those that a mesh axis runs over, the one named last changes fastest.
Arguments:
- positions: float32 [32, 3, 8, 3, 128], P('gx', 'gy', 'gz'), may hold values from 0 to 3
- features: bfloat16 [32, 3, 8, 128, 576], P('gx', 'gy', 'gz'), may hold values from -6 to 6
- species: int32 [32, 3, 8, 128], P('gx', 'gy', 'gz'), may hold values from 0 to 1
- neighbours: int32 [32, 3, 8, 12, 128], P('gx', 'gy', 'gz'), may hold values from 0 to 1855, as said below
- send_list: int32 [32, 3, 8, 64], P('gx', 'gy', 'gz'), may hold values from 0 to 127, as said below
- mix_weight: bfloat16 [3, 64, 64], replicated, may hold values from -0.75 to 0.75
- radial_in: float32 [8, 64], replicated, may hold values from -2 to 2
- radial_out: float32 [64, 192], replicated, may hold values from -3 to 3
- readout: float32 [2, 3, 64], replicated, may hold values from -0.1875 to 0.1875
Outputs:
- atom_energy: float32 [32, 3, 8, 128], P('gx', 'gy', 'gz')
- forces: float32 [32, 3, 8, 3, 128], P('gx', 'gy', 'gz')
- feature_grad: float32 [32, 3, 8, 128, 576], P('gx', 'gy', 'gz')
Inputs may be any that keep to these rules, and one draw needn't show every extreme that they name: `neighbours`: an entry below 128 is an own atom; an entry 128 + b * 64 + s is slot s of direction b, and b is never 13. `send_list`: the 64 entries of one brick are distinct.
All inputs are finite; a program needn't handle non-finite values.
Results may differ from a plain program's by a relative error of at most 0.0038.
Values may be sent and summed in bfloat16 or wider, within the bound.
A program may use at most 32 MiB of HBM per device.

v0:
```python
import math

import jax
import jax.numpy as jnp
from jax import lax
from jax.sharding import PartitionSpec as P

EDGE = 3.0
HIGH = lax.Precision.HIGHEST
LEVELS = (0, 1, 1, 1, 2, 2, 2, 2, 2)
ROOT_THREE = math.sqrt(3.0)
ROOT_FIVE = math.sqrt(5.0)
ROOT_FIFTEEN = math.sqrt(15.0)


def for_sending(value):

    def short(part):
        return part.astype(jnp.bfloat16) if part.dtype == jnp.float32 else part

    return jax.tree.map(short, value)


def passed_along(value, axis, steps):
    count = lax.axis_size(axis)
    pairs = [(source, (source + steps) % count) for source in range(count)]
    return lax.ppermute(value, axis, pairs)


def padded(cells, sides, width):
    for axis, dim in sides:
        count = lax.axis_size(axis)
        head = lax.slice_in_dim(cells, 0, width, axis=dim)
        tail = lax.slice_in_dim(cells, cells.shape[dim] - width, cells.shape[dim], axis=dim)
        cells = jnp.concatenate(
            [
                lax.ppermute(tail, axis, [(i, (i + 1) % count) for i in range(count)]),
                cells,
                lax.ppermute(head, axis, [((i + 1) % count, i) for i in range(count)]),
            ],
            axis=dim,
        )
    return cells


def harmonics(direction):
    comp_x, comp_y, comp_z = (direction[0], direction[1], direction[2])
    return jnp.stack(
        [
            jnp.ones_like(comp_x),
            ROOT_THREE * comp_x,
            ROOT_THREE * comp_y,
            ROOT_THREE * comp_z,
            ROOT_FIFTEEN * comp_x * comp_y,
            ROOT_FIFTEEN * comp_y * comp_z,
            0.5 * ROOT_FIVE * (2.0 * comp_z * comp_z - comp_x * comp_x - comp_y * comp_y),
            ROOT_FIFTEEN * comp_x * comp_z,
            0.5 * ROOT_FIFTEEN * (comp_x * comp_x - comp_y * comp_y),
        ]
    )


def geometry(displace, radial_in, radial_out):
    radius = jnp.sqrt(jnp.sum(displace * displace, 0) + 1.0)
    direction = displace / radius
    centres = 1.25 * jnp.arange(radial_in.shape[0]).astype(radius.dtype)
    spacing = radius[None, :] - centres[:, None]
    basis_set = jnp.exp(-0.5 * spacing * spacing)
    hidden = jax.nn.silu(jnp.dot(radial_in.T, basis_set, precision=HIGH))
    radial = lax.dot_general(hidden, radial_out, (((0,), (0,)), ((), ())), precision=HIGH)
    return (harmonics(direction), radial)


def spread(radial):
    atom_count = radial.shape[0]
    channels = radial.shape[1] // 3
    pieces = radial.reshape(atom_count, 3, channels)
    return jnp.concatenate(
        [
            pieces[:, 0:1],
            jnp.broadcast_to(pieces[:, 1:2], (atom_count, 3, channels)),
            jnp.broadcast_to(pieces[:, 2:3], (atom_count, 5, channels)),
        ],
        1,
    )


def offsets():
    direction_id = jnp.arange(27)
    return EDGE * jnp.stack(
        [direction_id // 9 - 1, direction_id // 3 % 3 - 1, direction_id % 3 - 1], 1
    ).astype(jnp.float32)


def local_layer(table_g, table_pos, own_pos, species, neighbours, radial_in, radial_out, readout):
    atom_count = own_pos.shape[1]
    slots = neighbours.shape[0]
    width = table_g.shape[1]
    channels = width // 9
    norm_scale = 1.0 / math.sqrt(slots)
    flat_index = neighbours.reshape(slots * atom_count)
    gathered_all = jnp.take(table_g, flat_index, axis=0).reshape(slots, atom_count, width)
    places_all = jnp.take(table_pos, flat_index, axis=1).reshape(3, slots, atom_count)
    displace_all = jnp.transpose(places_all, (1, 0, 2)) - own_pos[None]

    def forward_step(running, slot_pair):
        rows_bf, displace = slot_pair
        gathered = rows_bf.astype(jnp.float32).reshape(atom_count, 9, channels)
        harmonic, radial = geometry(displace, radial_in, radial_out)
        radial_full = spread(radial)
        message = radial_full * (harmonic.T[:, :, None] * gathered[:, 0:1, :] + gathered)
        return (running + message, None)

    summed, _ = lax.scan(
        forward_step,
        jnp.zeros((atom_count, 9, channels), jnp.float32),
        (gathered_all, displace_all),
    )
    accum = summed * norm_scale
    weights = jnp.where(species[:, None, None] == 1, readout[1][None], readout[0][None])
    square_one = jnp.sum(accum[:, 1:4] * accum[:, 1:4], 1)
    square_two = jnp.sum(accum[:, 4:9] * accum[:, 4:9], 1)
    energy = jnp.sum(
        weights[:, 0] * accum[:, 0] + weights[:, 1] * square_one + weights[:, 2] * square_two, -1
    )
    d_accum = (
        jnp.concatenate(
            [
                weights[:, 0:1],
                2.0 * weights[:, 1:2] * accum[:, 1:4],
                2.0 * weights[:, 2:3] * accum[:, 4:9],
            ],
            1,
        )
        * norm_scale
    )

    def backward_step(carry_none, slot_pair):
        rows_bf, displace = slot_pair
        gathered = rows_bf.astype(jnp.float32).reshape(atom_count, 9, channels)
        (harmonic, radial), pullback = jax.vjp(
            lambda moved: geometry(moved, radial_in, radial_out), displace
        )
        radial_full = spread(radial)
        harmonic_t = harmonic.T[:, :, None]
        coupled = harmonic_t * gathered[:, 0:1, :] + gathered
        weighted = d_accum * radial_full
        d_rows = weighted.at[:, 0].add(jnp.sum(weighted * harmonic_t, 1))
        d_full = d_accum * coupled
        d_radial = jnp.concatenate(
            [d_full[:, 0], jnp.sum(d_full[:, 1:4], 1), jnp.sum(d_full[:, 4:9], 1)], 1
        )
        d_harmonic = jnp.sum(weighted * gathered[:, 0:1, :], 2).T
        (d_displace,) = pullback((d_harmonic, d_radial))
        return (carry_none, (d_rows.reshape(atom_count, width), d_displace))

    _, (rows_grad, displace_grad) = lax.scan(backward_step, 0.0, (gathered_all, displace_all))
    rows_total = table_g.shape[0]
    grad_g = (
        jnp.zeros((rows_total, width), jnp.float32)
        .at[flat_index]
        .add(rows_grad.reshape(slots * atom_count, width))
    )
    spread_pos = jnp.transpose(displace_grad, (1, 0, 2)).reshape(3, slots * atom_count)
    grad_pos = jnp.zeros((3, rows_total), jnp.float32).at[:, flat_index].add(spread_pos)
    grad_pos = grad_pos.at[:, :atom_count].add(-jnp.sum(displace_grad, 0))
    return (energy, grad_g, grad_pos)


def move_x(blocks, offset_step):
    return jax.tree.map(
        lambda part, own: part.astype(own.dtype),
        passed_along(for_sending(blocks), "gx", offset_step),
        blocks,
    )


def move_y(blocks, offset_step):
    return jax.tree.map(
        lambda part, own: part.astype(own.dtype),
        passed_along(for_sending(blocks), "gy", offset_step),
        blocks,
    )


def move_z(blocks, offset_step):
    return jax.tree.map(
        lambda part, own: part.astype(own.dtype),
        passed_along(for_sending(blocks), "gz", offset_step),
        blocks,
    )


def fold(blocks, axis_dim, mover_fn):
    upper_part = tuple(
        (lax.index_in_dim(member, 2, axis_dim, False).astype(jnp.bfloat16) for member in blocks)
    )
    lower_part = tuple(
        (lax.index_in_dim(member, 0, axis_dim, False).astype(jnp.bfloat16) for member in blocks)
    )
    middle = tuple((lax.index_in_dim(member, 1, axis_dim, False) for member in blocks))
    came_up = mover_fn(upper_part, 1)
    came_down = mover_fn(lower_part, -1)
    return tuple(
        (
            centre + first.astype(jnp.float32) + second.astype(jnp.float32)
            for centre, first, second in zip(middle, came_up, came_down)
        )
    )


def shards(
    positions, features, species, neighbours, send_list, mix_weight, radial_in, radial_out, readout
):
    own_pos = positions[0, 0, 0]
    own_feat = features[0, 0, 0]
    kinds = species[0, 0, 0]
    slot_lists = neighbours[0, 0, 0]
    sending = send_list[0, 0, 0]
    atom_count = own_pos.shape[1]
    width = own_feat.shape[1]
    channels = width // 9
    send_count = sending.shape[0]
    expanded = mix_weight[jnp.array(LEVELS)]
    mixed = (
        jnp.einsum(
            "amd,mde->ame",
            own_feat.reshape(atom_count, 9, channels),
            expanded,
            preferred_element_type=jnp.float32,
        )
        .reshape(atom_count, width)
        .astype(jnp.bfloat16)
    )
    shared_g = jnp.take(mixed, sending, axis=0)[None, None, None]
    shared_pos = jnp.take(own_pos, sending, axis=1)[None, None, None]
    ghost_g = padded(shared_g, (("gx", 0), ("gy", 1), ("gz", 2)), 1)
    ghost_pos = padded(shared_pos, (("gx", 0), ("gy", 1), ("gz", 2)), 1)
    ghost_pos = ghost_pos.reshape(27, 3, send_count) + offsets()[:, :, None]
    table_g = jnp.concatenate([mixed, ghost_g.reshape(27 * send_count, width)], 0)
    table_pos = jnp.concatenate(
        [own_pos, jnp.transpose(ghost_pos, (1, 0, 2)).reshape(3, 27 * send_count)], 1
    )
    energy, grad_g, grad_pos = local_layer(
        table_g, table_pos, own_pos, kinds, slot_lists, radial_in, radial_out, readout
    )
    part_g = grad_g[atom_count:].reshape(3, 3, 3, send_count, width)
    part_pos = jnp.transpose(
        grad_pos[:, atom_count:].reshape(3, 27, send_count), (1, 0, 2)
    ).reshape(3, 3, 3, 3, send_count)
    blocks = (part_g, part_pos)
    blocks = fold(blocks, 2, move_z)
    blocks = fold(blocks, 1, move_y)
    blocks = fold(blocks, 0, move_x)
    returned_g, returned_pos = blocks
    own_g = grad_g[:atom_count].at[sending].add(returned_g)
    own_grad = grad_pos[:, :atom_count].at[:, sending].add(returned_pos)
    feature_grad = jnp.einsum(
        "ame,mde->amd",
        own_g.reshape(atom_count, 9, channels),
        expanded.astype(jnp.float32),
        precision=HIGH,
    ).reshape(atom_count, width)
    return (energy[None, None, None], (-own_grad)[None, None, None], feature_grad[None, None, None])


def solution(mesh):
    in_specs = (
        P("gx", "gy", "gz", None, None),
        P("gx", "gy", "gz", None, None),
        P("gx", "gy", "gz", None),
        P("gx", "gy", "gz", None, None),
        P("gx", "gy", "gz", None),
        P(),
        P(),
        P(),
        P(),
    )
    out_specs = (
        P("gx", "gy", "gz", None),
        P("gx", "gy", "gz", None, None),
        P("gx", "gy", "gz", None, None),
    )
    return jax.shard_map(shards, mesh=mesh, in_specs=in_specs, out_specs=out_specs, check_vma=False)
```

profile of v0, /device:TPU:6, one launch (start us, length us, event | category | flops | bytes accessed | tf_op | source)
XLA Modules:
  0.0 273.0 jit_solution(903727637753773333)
XLA Ops:
  3.5 10.8 %collective-permute-start.1 = (f32[1,1,1,3,64]{3,4,2,1,0:T(8,128)S(1)}, f32[1,1,1,3,64]{3,4,2,1,0:T(8,128)S(1)}, u32[]{:S(2)}, u32[]{:S(2)}) collective-permute-start(f32[1,1,1,3,64]{3,4,2,1,0:T(8,128)S(1)} %bitcast_select_fusion.1), channel_id=1, source_target_pairs={{24,0},{48,24},{72,48},{96,72},{120,96},{144,120},{168,144},{192,1... | collective-permute-start | bytes 2312 | tf_op jit(solution)/shard_map/ppermute | solution.py:39
  14.3 1.9 collective-permute-start
  19.5 7.8 %collective-permute-start.7 = (bf16[1,1,1,64,576]{4,3,2,1,0:T(8,128)(2,1)S(1)}, bf16[1,1,1,64,576]{4,3,2,1,0:T(8,128)(2,1)S(1)}, u32[]{:S(2)}, u32[]{:S(2)}) collective-permute-start(bf16[1,1,1,64,576]{4,3,2,1,0:T(8,128)(2,1)S(1)} %bitcast_select_fusion), channel_id=1, source_target_pairs={{24,0},{48,24},{72,48},{96,72},{120,96},{144,120},{168,144},{192,1... | collective-permute-start | bytes 221192 | tf_op jit(solution)/shard_map/ppermute | solution.py:39
  27.3 1.9 collective-permute-start.6
  33.1 11.9 %collective-permute-start.3 = (f32[3,1,1,3,64]{4,2,3,1,0:T(1,128)S(1)}, f32[3,1,1,3,64]{4,2,3,1,0:T(1,128)S(1)}, u32[]{:S(2)}, u32[]{:S(2)}) collective-permute-start(f32[3,1,1,3,64]{4,2,3,1,0:T(1,128)S(1)} %pad_maximum_fusion.7), channel_id=1, source_target_pairs={{8,0},{16,8},{0,16},{9,1},{17,9},{1,17},{10,2},{18,10},{2,18},{11,... | collective-permute-start | bytes 6920 | tf_op jit(solution)/shard_map/ppermute | solution.py:39
  45.0 1.9 collective-permute-start.2
  47.0 7.5 %collective-permute-done.2 = f32[3,1,1,3,64]{4,2,3,1,0:T(1,128)S(1)} collective-permute-done((f32[3,1,1,3,64]{4,2,3,1,0:T(1,128)S(1)}, f32[3,1,1,3,64]{4,2,3,1,0:T(1,128)S(1)}, u32[]{:S(2)}, u32[]{:S(2)}) %collective-permute-start.2) | collective-permute-done | bytes 2336 | tf_op jit(solution)/shard_map/ppermute | solution.py:37
  55.0 3.6 %collective-permute-start.9 = (bf16[3,1,1,64,576]{4,3,2,1,0:T(8,128)(2,1)S(1)}, bf16[3,1,1,64,576]{4,3,2,1,0:T(8,128)(2,1)S(1)}, u32[]{:S(2)}, u32[]{:S(2)}) collective-permute-start(bf16[3,1,1,64,576]{4,3,2,1,0:T(8,128)(2,1)S(1)} %pad_maximum_fusion.4), channel_id=1, source_target_pairs={{8,0},{16,8},{0,16},{9,1},{17,9},{1,17},{10,2},{18,10},{2,18},{11,... | collective-permute-start | bytes 663560 | tf_op jit(solution)/shard_map/ppermute | solution.py:39
  58.7 6.1 %collective-permute-start.8 = (bf16[3,1,1,64,576]{4,3,2,1,0:T(8,128)(2,1)S(1)}, bf16[3,1,1,64,576]{4,3,2,1,0:T(8,128)(2,1)S(1)}, u32[]{:S(2)}, u32[]{:S(2)}) collective-permute-start(bf16[3,1,1,64,576]{4,3,2,1,0:T(8,128)(2,1)S(1)} %pad_maximum_fusion.4), channel_id=1, source_target_pairs={{0,8},{8,16},{16,0},{1,9},{9,17},{17,1},{2,10},{10,18},{18,2},{3,1... | collective-permute-start | bytes 663560 | tf_op jit(solution)/shard_map/ppermute | solution.py:37
  66.6 8.3 %collective-permute-done.9 = bf16[3,1,1,64,576]{4,3,2,1,0:T(8,128)(2,1)S(1)} collective-permute-done((bf16[3,1,1,64,576]{4,3,2,1,0:T(8,128)(2,1)S(1)}, bf16[3,1,1,64,576]{4,3,2,1,0:T(8,128)(2,1)S(1)}, u32[]{:S(2)}, u32[]{:S(2)}) %collective-permute-start.9) | collective-permute-done | bytes 221216 | tf_op jit(solution)/shard_map/ppermute | solution.py:39
  75.0 8.0 %collective-permute-done.8 = bf16[3,1,1,64,576]{4,3,2,1,0:T(8,128)(2,1)S(1)} collective-permute-done((bf16[3,1,1,64,576]{4,3,2,1,0:T(8,128)(2,1)S(1)}, bf16[3,1,1,64,576]{4,3,2,1,0:T(8,128)(2,1)S(1)}, u32[]{:S(2)}, u32[]{:S(2)}) %collective-permute-start.8) | collective-permute-done | bytes 221216 | tf_op jit(solution)/shard_map/ppermute | solution.py:37
  86.3 3.8 %gather_fusion.1 = f32[1536,3]{1,0:T(8,128)S(1)} fusion(f32[3,1856]{0,1:T(8,128)} %pad_maximum_fusion.2, s32[2048]{0:T(1024)S(1)} %pad_clamp_fusion), kind=kCustom, calls=%fused_computation.1 | custom fusion | bytes 43008 | tf_op jit(solution)/shard_map/jit(_take)/gather | solution.py:103
  90.4 4.1 %collective-permute-done.11 = bf16[3,3,1,64,576]{4,3,2,1,0:T(8,128)(2,1)} collective-permute-done((bf16[3,3,1,64,576]{4,3,2,1,0:T(8,128)(2,1)}, bf16[3,3,1,64,576]{4,3,2,1,0:T(8,128)(2,1)}, u32[]{:S(2)}, u32[]{:S(2)}) %collective-permute-start.11) | collective-permute-done | bytes 663584 | tf_op jit(solution)/shard_map/ppermute | solution.py:39
  98.7 5.6 %gather_fusion.4 = bf16[1536,576]{1,0:T(8,128)(2,1)} fusion(bf16[1856,576]{1,0:T(8,128)(2,1)S(1)} %pad_maximum_fusion, s32[2048]{0:T(1024)S(1)} %copy-done.5), kind=kCustom, calls=%fused_computation.4 | custom fusion | bytes 3545088 | tf_op jit(solution)/shard_map/jit(_take)/gather | solution.py:102
  104.3 2.8 %copy.145 = bf16[12,128,576]{1,2,0:T(8,128)(2,1)S(1)} copy(bf16[12,128,576]{2,1,0:T(8,128)(2,1)} %bitcast.296) | data formatting | bytes 3538944 | tf_op jit(solution)/shard_map/jit(_take)/gather | solution.py:102
  108.5 23.1 %while.28 = (s32[]{:T(128)}, f32[128,9,64]{0,2,1:T(8,128)S(1)}, f32[12,3,128]{2,1,0:T(4,128)S(1)}, f32[8,64]{1,0:T(8,128)S(1)}, f32[64,192]{1,0:T(8,128)S(1)}, /...) while((s32[]{:T(128)}, f32[128,9,64]{0,2,1:T(8,128)S(1)}, ...), condition=%wide.region_2.3_spmd.clone, body=%wide.region_0.0_spmd.clone.sunk | while | flops 20363536 | bytes 2634431 | solution.py:114
  131.8 38.4 %while.27 = (s32[]{:T(128)}, f32[12,128,576]{1,2,0:T(8,128)}, f32[12,3,128]{2,1,0:T(4,128)S(1)}, f32[12,3,128]{2,1,0:T(4,128)S(1)}, f32[8,64]{1,0:T(8,128)S(1)},...) while((s32[]{:T(128)}, f32[12,128,576]{1,2,0:T(8,128)}, ...), condition=%wide.region_15.16_spmd, body=%wide.region_7.15_spmd.sunk | while | flops 40436240 | bytes 4321001 | solution.py:157
  170.3 5.4 %copy.158 = f32[12,128,576]{2,1,0:T(8,128)} copy(f32[12,128,576]{1,2,0:T(8,128)} %get-tuple-element.163) | data formatting | bytes 7077888 | tf_op jit(solution)/shard_map/while | solution.py:157
  176.0 9.3 %scatter_custom_fusion = f32[3,1856]{0,1:T(8,128)S(1)} fusion(s32[1536]{0:T(1024)} %copy-done.7, f32[1536,3]{1,0:T(8,128)S(1)} %copy.146, f32[]{:T(128)} %constant.260.clone.1), kind=kCustom, calls=%fused_computation.154 | custom fusion | flops 4608 | bytes 22784 | tf_op jit(solution)/shard_map/scatter-add | solution.py:165
  186.4 13.5 %scatter_custom_fusion.2 = f32[1856,576]{1,0:T(8,128)} fusion(s32[1536]{0:T(1024)} %copy-done.7, f32[1536,576]{1,0:T(8,128)} %bitcast.297, f32[]{:T(128)} %constant.260.clone.1), kind=kCustom, calls=%fused_computation.139 | custom fusion | flops 884736 | bytes 4276736 | tf_op jit(solution)/shard_map/scatter-add | solution.py:162
  199.9 2.5 slice.312
  202.9 2.5 collective-permute-start.18
  206.1 7.6 %collective-permute-start.15 = (bf16[3,3,64]{2,0,1:T(4,128)(2,1)S(1)}, bf16[3,3,64]{2,0,1:T(4,128)(2,1)S(1)}, u32[]{:S(2)}, u32[]{:S(2)}) collective-permute-start(bf16[3,3,64]{2,0,1:T(4,128)(2,1)S(1)} %bitcast.317), channel_id=1, source_target_pairs={{0,16},{8,0},{16,8},{1,17},{9,1},{17,9},{2,18},{10,2},{18,10},{3,1... | collective-permute-start | bytes 3464 | tf_op jit(solution)/shard_map/ppermute | solution.py:27
  213.6 2.2 collective-permute-start.14
  216.4 6.6 %collective-permute-done.14 = bf16[3,3,64]{2,0,1:T(4,128)(2,1)S(1)} collective-permute-done((bf16[3,3,64]{2,0,1:T(4,128)(2,1)S(1)}, bf16[3,3,64]{2,0,1:T(4,128)(2,1)S(1)}, u32[]{:S(2)}, u32[]{:S(2)}) %collective-permute-start.14) | collective-permute-done | bytes 1184 | tf_op jit(solution)/shard_map/ppermute | solution.py:27
  225.0 3.9 %collective-permute-start.16 = (bf16[3,64]{1,0:T(4,128)(2,1)S(1)}, bf16[3,64]{1,0:T(4,128)(2,1)S(1)}, u32[]{:S(2)}, u32[]{:S(2)}) collective-permute-start(bf16[3,64]{1,0:T(4,128)(2,1)S(1)} %bitcast.318), channel_id=1, source_target_pairs={{0,24},{24,48},{48,72},{72,96},{96,120},{120,144},{144,168},{168,1... | collective-permute-start | bytes 1160 | tf_op jit(solution)/shard_map/ppermute | solution.py:27
  229.3 2.3 collective-permute-start.20
  231.7 7.6 %collective-permute-start.21 = (bf16[3,64,576]{2,1,0:T(8,128)(2,1)S(1)}, bf16[3,64,576]{2,1,0:T(8,128)(2,1)S(1)}, u32[]{:S(2)}, u32[]{:S(2)}) collective-permute-start(bf16[3,64,576]{2,1,0:T(8,128)(2,1)S(1)} %get-tuple-element.272), channel_id=1, source_target_pairs={{0,16},{8,0},{16,8},{1,17},{9,1},{17,9},{2,18},{10,2},{18,10},{3,1... | collective-permute-start | bytes 663560 | tf_op jit(solution)/shard_map/ppermute | solution.py:27
  240.3 7.4 %collective-permute-done.20 = bf16[3,64,576]{2,1,0:T(8,128)(2,1)S(1)} collective-permute-done((bf16[3,64,576]{2,1,0:T(8,128)(2,1)S(1)}, bf16[3,64,576]{2,1,0:T(8,128)(2,1)S(1)}, u32[]{:S(2)}, u32[]{:S(2)}) %collective-permute-start.20) | collective-permute-done | bytes 221216 | tf_op jit(solution)/shard_map/ppermute | solution.py:27
  247.7 2.9 %collective-permute-done.21 = bf16[3,64,576]{2,1,0:T(8,128)(2,1)S(1)} collective-permute-done((bf16[3,64,576]{2,1,0:T(8,128)(2,1)S(1)}, bf16[3,64,576]{2,1,0:T(8,128)(2,1)S(1)}, u32[]{:S(2)}, u32[]{:S(2)}) %collective-permute-start.21) | collective-permute-done | bytes 221216 | tf_op jit(solution)/shard_map/ppermute | solution.py:27
  252.4 5.4 %collective-permute-start.22 = (bf16[64,576]{1,0:T(8,128)(2,1)S(1)}, bf16[64,576]{1,0:T(8,128)(2,1)S(1)}, u32[]{:S(2)}, u32[]{:S(2)}) collective-permute-start(bf16[64,576]{1,0:T(8,128)(2,1)S(1)} %get-tuple-element.277), channel_id=1, source_target_pairs={{0,24},{24,48},{48,72},{72,96},{96,120},{120,144},{144,168},{168,1... | collective-permute-start | bytes 221192 | tf_op jit(solution)/shard_map/ppermute | solution.py:27
  257.8 10.8 %collective-permute-start.23 = (bf16[64,576]{1,0:T(8,128)(2,1)S(1)}, bf16[64,576]{1,0:T(8,128)(2,1)S(1)}, u32[]{:S(2)}, u32[]{:S(2)}) collective-permute-start(bf16[64,576]{1,0:T(8,128)(2,1)S(1)} %get-tuple-element.278), channel_id=1, source_target_pairs={{0,744},{24,0},{48,24},{72,48},{96,72},{120,96},{144,120},{168,144... | collective-permute-start | bytes 221192 | tf_op jit(solution)/shard_map/ppermute | solution.py:27
  (670 shorter events, 92.4 us)
Async XLA Ops:
  0.6 17.6 %copy-start = (bf16[1,1,1,128,576]{3,4,2,1,0:T(8,128)(2,1)S(1)}, bf16[1,1,1,128,576]{3,4,2,1,0:T(8,128)(2,1)}, u32[]{:S(2)}) copy-start(bf16[1,1,1,128,576]{3,4,2,1,0:T(8,128)(2,1)} %param.19) | copy-start | bytes 442372
  1.3 12.9 %copy-start.10 = (s32[64]{0:T(128)}, s32[64]{0:T(128)S(1)}, u32[]{:S(2)}) copy-start(s32[64]{0:T(128)S(1)} %fusion.94) | copy-start | bytes 772
  3.5 29.5 %collective-permute-start.1 = (f32[1,1,1,3,64]{3,4,2,1,0:T(8,128)S(1)}, f32[1,1,1,3,64]{3,4,2,1,0:T(8,128)S(1)}, u32[]{:S(2)}, u32[]{:S(2)}) collective-permute-start(f32[1,1,1,3,64]{3,4,2,1,0:T(8,128)S(1)} %bitcast_select_fusion.1), channel_id=1, source_target_pairs={{24,0},{48,24},{72,48},{96,72},{120,96},{144,120},{168,144},{192,1... | collective-permute-start | bytes 2312 | tf_op jit(solution)/shard_map/ppermute | solution.py:39
  14.3 18.7 %collective-permute-start = (f32[1,1,1,3,64]{3,4,2,1,0:T(8,128)S(1)}, f32[1,1,1,3,64]{3,4,2,1,0:T(8,128)S(1)}, u32[]{:S(2)}, u32[]{:S(2)}) collective-permute-start(f32[1,1,1,3,64]{3,4,2,1,0:T(8,128)S(1)} %bitcast_select_fusion.1), channel_id=1, source_target_pairs={{0,24},{24,48},{48,72},{72,96},{96,120},{120,144},{144,168},{168,1... | collective-permute-start | bytes 2312 | tf_op jit(solution)/shard_map/ppermute | solution.py:37
  19.5 35.5 %collective-permute-start.7 = (bf16[1,1,1,64,576]{4,3,2,1,0:T(8,128)(2,1)S(1)}, bf16[1,1,1,64,576]{4,3,2,1,0:T(8,128)(2,1)S(1)}, u32[]{:S(2)}, u32[]{:S(2)}) collective-permute-start(bf16[1,1,1,64,576]{4,3,2,1,0:T(8,128)(2,1)S(1)} %bitcast_select_fusion), channel_id=1, source_target_pairs={{24,0},{48,24},{72,48},{96,72},{120,96},{144,120},{168,144},{192,1... | collective-permute-start | bytes 221192 | tf_op jit(solution)/shard_map/ppermute | solution.py:39
  27.3 27.6 %collective-permute-start.6 = (bf16[1,1,1,64,576]{4,3,2,1,0:T(8,128)(2,1)S(1)}, bf16[1,1,1,64,576]{4,3,2,1,0:T(8,128)(2,1)S(1)}, u32[]{:S(2)}, u32[]{:S(2)}) collective-permute-start(bf16[1,1,1,64,576]{4,3,2,1,0:T(8,128)(2,1)S(1)} %bitcast_select_fusion), channel_id=1, source_target_pairs={{0,24},{24,48},{48,72},{72,96},{96,120},{120,144},{144,168},{168,1... | collective-permute-start | bytes 221192 | tf_op jit(solution)/shard_map/ppermute | solution.py:37
  32.7 53.7 %copy-start.4 = (s32[2048]{0:T(1024)}, s32[2048]{0:T(1024)S(1)}, u32[]{:S(2)}) copy-start(s32[2048]{0:T(1024)S(1)} %pad_clamp_fusion) | copy-start | bytes 24580
  33.1 13.8 %collective-permute-start.3 = (f32[3,1,1,3,64]{4,2,3,1,0:T(1,128)S(1)}, f32[3,1,1,3,64]{4,2,3,1,0:T(1,128)S(1)}, u32[]{:S(2)}, u32[]{:S(2)}) collective-permute-start(f32[3,1,1,3,64]{4,2,3,1,0:T(1,128)S(1)} %pad_maximum_fusion.7), channel_id=1, source_target_pairs={{8,0},{16,8},{0,16},{9,1},{17,9},{1,17},{10,2},{18,10},{2,18},{11,... | collective-permute-start | bytes 6920 | tf_op jit(solution)/shard_map/ppermute | solution.py:39
  45.0 9.4 %collective-permute-start.2 = (f32[3,1,1,3,64]{4,2,3,1,0:T(1,128)S(1)}, f32[3,1,1,3,64]{4,2,3,1,0:T(1,128)S(1)}, u32[]{:S(2)}, u32[]{:S(2)}) collective-permute-start(f32[3,1,1,3,64]{4,2,3,1,0:T(1,128)S(1)} %pad_maximum_fusion.7), channel_id=1, source_target_pairs={{0,8},{8,16},{16,0},{1,9},{9,17},{17,1},{2,10},{10,18},{18,2},{3,1... | collective-permute-start | bytes 6920 | tf_op jit(solution)/shard_map/ppermute | solution.py:37
  54.4 11.8 %collective-permute-start.5 = (f32[3,3,1,3,64]{4,2,3,1,0:T(1,128)S(1)}, f32[3,3,1,3,64]{4,2,3,1,0:T(1,128)S(1)}, u32[]{:S(2)}, u32[]{:S(2)}) collective-permute-start(f32[3,3,1,3,64]{4,2,3,1,0:T(1,128)S(1)} %pad_maximum_fusion.6), channel_id=1, source_target_pairs={{1,0},{2,1},{3,2},{4,3},{5,4},{6,5},{7,6},{0,7},{9,8},{10,9},{11,1... | collective-permute-start | bytes 20744 | tf_op jit(solution)/shard_map/ppermute | solution.py:39
  54.5 11.8 %collective-permute-start.4 = (f32[3,3,1,3,64]{4,2,3,1,0:T(1,128)S(1)}, f32[3,3,1,3,64]{4,2,3,1,0:T(1,128)S(1)}, u32[]{:S(2)}, u32[]{:S(2)}) collective-permute-start(f32[3,3,1,3,64]{4,2,3,1,0:T(1,128)S(1)} %pad_maximum_fusion.6), channel_id=1, source_target_pairs={{0,1},{1,2},{2,3},{3,4},{4,5},{5,6},{6,7},{7,0},{8,9},{9,10},{10,1... | collective-permute-start | bytes 20744 | tf_op jit(solution)/shard_map/ppermute | solution.py:37
  55.0 20.0 %collective-permute-start.9 = (bf16[3,1,1,64,576]{4,3,2,1,0:T(8,128)(2,1)S(1)}, bf16[3,1,1,64,576]{4,3,2,1,0:T(8,128)(2,1)S(1)}, u32[]{:S(2)}, u32[]{:S(2)}) collective-permute-start(bf16[3,1,1,64,576]{4,3,2,1,0:T(8,128)(2,1)S(1)} %pad_maximum_fusion.4), channel_id=1, source_target_pairs={{8,0},{16,8},{0,16},{9,1},{17,9},{1,17},{10,2},{18,10},{2,18},{11,... | collective-permute-start | bytes 663560 | tf_op jit(solution)/shard_map/ppermute | solution.py:39
  58.7 24.3 %collective-permute-start.8 = (bf16[3,1,1,64,576]{4,3,2,1,0:T(8,128)(2,1)S(1)}, bf16[3,1,1,64,576]{4,3,2,1,0:T(8,128)(2,1)S(1)}, u32[]{:S(2)}, u32[]{:S(2)}) collective-permute-start(bf16[3,1,1,64,576]{4,3,2,1,0:T(8,128)(2,1)S(1)} %pad_maximum_fusion.4), channel_id=1, source_target_pairs={{0,8},{8,16},{16,0},{1,9},{9,17},{17,1},{2,10},{10,18},{18,2},{3,1... | collective-permute-start | bytes 663560 | tf_op jit(solution)/shard_map/ppermute | solution.py:37
  66.3 19.0 %copy-start.6 = (f32[27,3]{1,0:T(8,128)S(1)}, f32[27,3]{1,0:T(8,128)}, u32[]{:S(2)}) copy-start(f32[27,3]{1,0:T(8,128)} %copy.138) | copy-start | bytes 976
  84.0 6.4 %copy-start.8 = (pred[12,128]{1,0:T(8,128)(4,1)S(1)}, pred[12,128]{1,0:T(8,128)(4,1)}, u32[]{:S(2)}) copy-start(pred[12,128]{1,0:T(8,128)(4,1)} %compare_and_fusion) | copy-start | bytes 4612
  84.0 10.5 %collective-permute-start.11 = (bf16[3,3,1,64,576]{4,3,2,1,0:T(8,128)(2,1)}, bf16[3,3,1,64,576]{4,3,2,1,0:T(8,128)(2,1)}, u32[]{:S(2)}, u32[]{:S(2)}) collective-permute-start(bf16[3,3,1,64,576]{4,3,2,1,0:T(8,128)(2,1)} %pad_maximum_fusion.3), channel_id=1, source_target_pairs={{1,0},{2,1},{3,2},{4,3},{5,4},{6,5},{7,6},{0,7},{9,8},{10,9},{11,1... | collective-permute-start | bytes 1990664 | tf_op jit(solution)/shard_map/ppermute | solution.py:39
  85.2 11.2 %collective-permute-start.10 = (bf16[3,3,1,64,576]{4,3,2,1,0:T(8,128)(2,1)}, bf16[3,3,1,64,576]{4,3,2,1,0:T(8,128)(2,1)}, u32[]{:S(2)}, u32[]{:S(2)}) collective-permute-start(bf16[3,3,1,64,576]{4,3,2,1,0:T(8,128)(2,1)} %pad_maximum_fusion.3), channel_id=1, source_target_pairs={{0,1},{1,2},{2,3},{3,4},{4,5},{5,6},{6,7},{7,0},{8,9},{9,10},{10,1... | collective-permute-start | bytes 1990664 | tf_op jit(solution)/shard_map/ppermute | solution.py:37
  108.5 23.2 %copy-start.3 = (f32[12,3,128]{2,1,0:T(4,128)S(1)}, f32[12,3,128]{2,1,0:T(4,128)}, u32[]{:S(2)}) copy-start(f32[12,3,128]{2,1,0:T(4,128)} %custom-call.12) | copy-start | bytes 55300
  185.8 20.1 %collective-permute-start.13 = (bf16[3,3,3,64]{3,1,0,2:T(4,128)(2,1)S(1)}, bf16[3,3,3,64]{3,1,0,2:T(4,128)(2,1)S(1)}, u32[]{:S(2)}, u32[]{:S(2)}) collective-permute-start(bf16[3,3,3,64]{3,1,0,2:T(4,128)(2,1)S(1)} %bitcast.315), channel_id=1, source_target_pairs={{0,7},{1,0},{2,1},{3,2},{4,3},{5,4},{6,5},{7,6},{8,15},{9,8},{10,9... | collective-permute-start | bytes 10376 | tf_op jit(solution)/shard_map/ppermute | solution.py:27
  186.2 19.8 %collective-permute-start.12 = (bf16[3,3,3,64]{3,1,0,2:T(4,128)(2,1)S(1)}, bf16[3,3,3,64]{3,1,0,2:T(4,128)(2,1)S(1)}, u32[]{:S(2)}, u32[]{:S(2)}) collective-permute-start(bf16[3,3,3,64]{3,1,0,2:T(4,128)(2,1)S(1)} %bitcast.314), channel_id=1, source_target_pairs={{0,1},{1,2},{2,3},{3,4},{4,5},{5,6},{6,7},{7,0},{8,9},{9,10},{10,1... | collective-permute-start | bytes 10376 | tf_op jit(solution)/shard_map/ppermute | solution.py:27
  202.9 26.0 %collective-permute-start.18 = (bf16[3,3,64,576]{3,2,1,0:T(8,128)(2,1)S(1)}, bf16[3,3,64,576]{3,2,1,0:T(8,128)(2,1)S(1)}, u32[]{:S(2)}, u32[]{:S(2)}) collective-permute-start(bf16[3,3,64,576]{3,2,1,0:T(8,128)(2,1)S(1)} %get-tuple-element.269), channel_id=1, source_target_pairs={{0,1},{1,2},{2,3},{3,4},{4,5},{5,6},{6,7},{7,0},{8,9},{9,10},{10,1... | collective-permute-start | bytes 1990664 | tf_op jit(solution)/shard_map/ppermute | solution.py:27
  205.4 23.6 %collective-permute-start.19 = (bf16[3,3,64,576]{3,2,1,0:T(8,128)(2,1)S(1)}, bf16[3,3,64,576]{3,2,1,0:T(8,128)(2,1)S(1)}, u32[]{:S(2)}, u32[]{:S(2)}) collective-permute-start(bf16[3,3,64,576]{3,2,1,0:T(8,128)(2,1)S(1)} %get-tuple-element.270), channel_id=1, source_target_pairs={{0,7},{1,0},{2,1},{3,2},{4,3},{5,4},{6,5},{7,6},{8,15},{9,8},{10,9... | collective-permute-start | bytes 1990664 | tf_op jit(solution)/shard_map/ppermute | solution.py:27
  206.1 10.3 %collective-permute-start.15 = (bf16[3,3,64]{2,0,1:T(4,128)(2,1)S(1)}, bf16[3,3,64]{2,0,1:T(4,128)(2,1)S(1)}, u32[]{:S(2)}, u32[]{:S(2)}) collective-permute-start(bf16[3,3,64]{2,0,1:T(4,128)(2,1)S(1)} %bitcast.317), channel_id=1, source_target_pairs={{0,16},{8,0},{16,8},{1,17},{9,1},{17,9},{2,18},{10,2},{18,10},{3,1... | collective-permute-start | bytes 3464 | tf_op jit(solution)/shard_map/ppermute | solution.py:27
  213.6 9.4 %collective-permute-start.14 = (bf16[3,3,64]{2,0,1:T(4,128)(2,1)S(1)}, bf16[3,3,64]{2,0,1:T(4,128)(2,1)S(1)}, u32[]{:S(2)}, u32[]{:S(2)}) collective-permute-start(bf16[3,3,64]{2,0,1:T(4,128)(2,1)S(1)} %bitcast.316), channel_id=1, source_target_pairs={{0,8},{8,16},{16,0},{1,9},{9,17},{17,1},{2,10},{10,18},{18,2},{3,1... | collective-permute-start | bytes 3464 | tf_op jit(solution)/shard_map/ppermute | solution.py:27
  223.1 16.2 %collective-permute-start.17 = (bf16[3,64]{1,0:T(4,128)(2,1)S(1)}, bf16[3,64]{1,0:T(4,128)(2,1)S(1)}, u32[]{:S(2)}, u32[]{:S(2)}) collective-permute-start(bf16[3,64]{1,0:T(4,128)(2,1)S(1)} %bitcast.319), channel_id=1, source_target_pairs={{0,744},{24,0},{48,24},{72,48},{96,72},{120,96},{144,120},{168,144... | collective-permute-start | bytes 1160 | tf_op jit(solution)/shard_map/ppermute | solution.py:27
  225.0 14.4 %copy-start.11 = (s32[64]{0:T(128)S(1)}, s32[64]{0:T(128)}, u32[]{:S(2)}) copy-start(s32[64]{0:T(128)} %copy-done.10) | copy-start | bytes 772
  225.0 14.2 %collective-permute-start.16 = (bf16[3,64]{1,0:T(4,128)(2,1)S(1)}, bf16[3,64]{1,0:T(4,128)(2,1)S(1)}, u32[]{:S(2)}, u32[]{:S(2)}) collective-permute-start(bf16[3,64]{1,0:T(4,128)(2,1)S(1)} %bitcast.318), channel_id=1, source_target_pairs={{0,24},{24,48},{48,72},{72,96},{96,120},{120,144},{144,168},{168,1... | collective-permute-start | bytes 1160 | tf_op jit(solution)/shard_map/ppermute | solution.py:27
  229.3 41.4 %slice-start = ((f32[1856,576]{1,0:T(8,128)}), f32[128,576]{1,0:T(8,128)S(1)}, s32[]{:S(2)}) async-start(f32[1856,576]{1,0:T(8,128)} %scatter_custom_fusion.2), calls=%async_computation | async-start | bytes 655360 | tf_op jit(solution)/shard_map/slice | solution.py:256
  229.3 18.4 %collective-permute-start.20 = (bf16[3,64,576]{2,1,0:T(8,128)(2,1)S(1)}, bf16[3,64,576]{2,1,0:T(8,128)(2,1)S(1)}, u32[]{:S(2)}, u32[]{:S(2)}) collective-permute-start(bf16[3,64,576]{2,1,0:T(8,128)(2,1)S(1)} %get-tuple-element.271), channel_id=1, source_target_pairs={{0,8},{8,16},{16,0},{1,9},{9,17},{17,1},{2,10},{10,18},{18,2},{3,1... | collective-permute-start | bytes 663560 | tf_op jit(solution)/shard_map/ppermute | solution.py:27
  231.7 19.0 %collective-permute-start.21 = (bf16[3,64,576]{2,1,0:T(8,128)(2,1)S(1)}, bf16[3,64,576]{2,1,0:T(8,128)(2,1)S(1)}, u32[]{:S(2)}, u32[]{:S(2)}) collective-permute-start(bf16[3,64,576]{2,1,0:T(8,128)(2,1)S(1)} %get-tuple-element.272), channel_id=1, source_target_pairs={{0,16},{8,0},{16,8},{1,17},{9,1},{17,9},{2,18},{10,2},{18,10},{3,1... | collective-permute-start | bytes 663560 | tf_op jit(solution)/shard_map/ppermute | solution.py:27
  252.4 16.9 %collective-permute-start.22 = (bf16[64,576]{1,0:T(8,128)(2,1)S(1)}, bf16[64,576]{1,0:T(8,128)(2,1)S(1)}, u32[]{:S(2)}, u32[]{:S(2)}) collective-permute-start(bf16[64,576]{1,0:T(8,128)(2,1)S(1)} %get-tuple-element.277), channel_id=1, source_target_pairs={{0,24},{24,48},{48,72},{72,96},{96,120},{120,144},{144,168},{168,1... | collective-permute-start | bytes 221192 | tf_op jit(solution)/shard_map/ppermute | solution.py:27
  257.8 12.8 %collective-permute-start.23 = (bf16[64,576]{1,0:T(8,128)(2,1)S(1)}, bf16[64,576]{1,0:T(8,128)(2,1)S(1)}, u32[]{:S(2)}, u32[]{:S(2)}) collective-permute-start(bf16[64,576]{1,0:T(8,128)(2,1)S(1)} %get-tuple-element.278), channel_id=1, source_target_pairs={{0,744},{24,0},{48,24},{72,48},{96,72},{120,96},{144,120},{168,144... | collective-permute-start | bytes 221192 | tf_op jit(solution)/shard_map/ppermute | solution.py:27
  (6 other events, 8.6 us)
where the time goes:
time: 275 us; the launch traced here: 273 us
  starting transfers between devices  92.5 us (34%)
  local copies, waits for them, and re-layouts  62.4 us (23%)
  waiting for transfers between devices  48.2 us (18%)
  other arithmetic  45.2 us (16%)
  matrix products  20.2 us (7%)
  loops' own time  3.11 us (1%)
    ppermute x12, starting transfers between devices, passed_along(): return lax.ppermute(value, axis, pairs)  44.7 us
    ppermute x6, starting transfers between devices, padded(): lax.ppermute(head, axis, [((i + 1) % count, i) for i in range(count)])  35.4 us
    dynamic_slice x24, local copies, waits for them, and re-layouts, local_layer(): lax.scan(forward_step, jnp.zeros((atom_count, 9, channels), jnp.float32),...  22.2 us
    ppermute x12, waiting for transfers between devices, passed_along(): return lax.ppermute(value, axis, pairs)  18.3 us
    ppermute x6, waiting for transfers between devices, padded(): lax.ppermute(tail, axis, [(i, (i + 1) % count) for i in range(count)])  17.4 us
    scatter-add x1, other arithmetic, local_layer(): grad_g = jnp.zeros((rows_total, width), jnp.float32).at[flat_index].add(r...  13.5 us
    ppermute x6, waiting for transfers between devices, padded(): lax.ppermute(head, axis, [((i + 1) % count, i) for i in range(count)])  12.5 us
    ppermute x6, starting transfers between devices, padded(): lax.ppermute(tail, axis, [(i, (i + 1) % count) for i in range(count)])  12.4 us
  transfers between devices with their start and end apart: 24, of which 9 were waited for; matrix products, arithmetic and copies ran while one was open for 12% of the time, Pallas kernels for 0%

commit v1 on v0

v1 whole, which is shorter than its diff:
```python
import math

import jax
import jax.numpy as jnp
from jax import lax
from jax.experimental import pallas as pl
from jax.experimental.pallas import tpu as pltpu
from jax.sharding import PartitionSpec as P

EDGE = 3.0
HIGH = lax.Precision.HIGHEST
MESH = pl.DeviceIdType.MESH
LEVELS = (0, 1, 1, 1, 2, 2, 2, 2, 2)
ROOT_THREE = math.sqrt(3.0)
ROOT_FIVE = math.sqrt(5.0)
ROOT_FIFTEEN = math.sqrt(15.0)

ATOMS = 128
SEND = 64
SLOTS = 12
EDGES = SLOTS * ATOMS
CH = 64
FEAT = 576
WIDE = 640
FLAT0 = 128
PAIR0 = 640
ROWS = 1792

NN = (((1,), (0,)), ((), ()))
NT = (((1,), (1,)), ((), ()))
TN = (((0,), (0,)), ((), ()))
F32 = jnp.float32
BF16 = jnp.bfloat16


def dot(lhs, rhs, dims=NN, precision=None):
    return lax.dot_general(lhs, rhs, dims, precision=precision, preferred_element_type=F32)


def column(dx, dy):
    return (dx + 1) * 3 + dy + 1


def row_of(dx, dy, dz):
    spot = column(dx, dy)
    if dz == 0:
        return FLAT0 + SEND * (spot - (spot > 4))
    return PAIR0 + 2 * SEND * spot + SEND * (dz > 0)


def code(dx, dy, dz):
    return column(dx, dy) * 3 + dz + 1


def eye(size):
    return jnp.where(
        lax.broadcasted_iota(jnp.int32, (size, size), 0)
        == lax.broadcasted_iota(jnp.int32, (size, size), 1),
        1.0,
        0.0,
    ).astype(BF16)


def parts(value):
    first = value.astype(BF16).astype(F32)
    rest = value - first
    second = rest.astype(BF16).astype(F32)
    third = rest - second
    filler = jnp.zeros((40, value.shape[1]), F32)
    return jnp.concatenate([first, second, third, filler], 0).astype(BF16)


def split(value):
    high = value.astype(BF16)
    return high, (value - high.astype(F32)).astype(BF16)


def mixers(mix_ref):
    zero = jnp.zeros((CH, CH), BF16)

    def pair(upper, lower):
        return jnp.concatenate(
            [
                jnp.concatenate([mix_ref[upper], zero], 1),
                jnp.concatenate([zero, mix_ref[lower]], 1),
            ],
            0,
        )

    last = pair(2, 2)
    return (pair(0, 1), pair(1, 1), last, last)


def kernel(
    pos_ref,
    feat_ref,
    spec_ref,
    nbr_ref,
    list_ref,
    mix_ref,
    rin_ref,
    rout_ref,
    read_ref,
    energy_ref,
    force_ref,
    fgrad_ref,
    tbl,
    tbl_t,
    shared,
    onehot,
    gath,
    placed,
    base,
    index,
    radial,
    pre,
    harm,
    accum,
    drows,
    dlow,
    drad,
    dharm,
    acc0,
    zsend,
    zrecv,
    xsend,
    xrecv,
    ysend,
    yrecv,
    fsend_sem,
    frecv_sem,
    bsend_sem,
    brecv_sem,
):
    size_x, size_y, size_z = (lax.axis_size(name) for name in ("gx", "gy", "gz"))
    me_x, me_y, me_z = (lax.axis_index(name) for name in ("gx", "gy", "gz"))

    def device(dx, dy, dz):
        return (
            lax.rem(me_x + dx + size_x, size_x),
            lax.rem(me_y + dy + size_y, size_y),
            lax.rem(me_z + dz + size_z, size_z),
        )

    sides = ((0, -1, 0), (0, 1, 0), (-1, 0, 0), (1, 0, 0), (0, 0, -1), (0, 0, 1))
    barrier = pltpu.get_barrier_semaphore()
    for side in sides:
        pl.semaphore_signal(barrier, inc=1, device_id=device(*side), device_id_type=MESH)

    mix = mixers(mix_ref)
    eye_big = eye(ATOMS)
    pos8 = jnp.concatenate([pos_ref[...], jnp.zeros((5, ATOMS), F32)], 0)
    pos_parts = parts(pos8)
    for tile in range(4):
        lanes = slice(128 * tile, 128 * tile + 128)
        tbl[0:ATOMS, lanes] = dot(feat_ref[:, lanes], mix[tile]).astype(BF16)
    tbl[0:ATOMS, 512:FEAT] = dot(feat_ref[:, 512:FEAT], mix_ref[2]).astype(BF16)
    tbl[0:ATOMS, FEAT:WIDE] = dot(eye_big, pos_parts, NT).astype(BF16)
    picks_t = jnp.where(
        lax.broadcasted_iota(jnp.int32, (ATOMS, SEND), 0) == list_ref[...], 1.0, 0.0
    ).astype(BF16)
    picks = dot(eye(SEND), picks_t, NT).astype(BF16)
    shared[...] = dot(picks, tbl[0:ATOMS, :]).astype(BF16)

    pl.semaphore_wait(barrier, len(sides))

    def halo(dx, dy, dz, axis):
        go = [0, 0, 0]
        go[axis] = -(dx, dy, dz)[axis]
        from_ = [dx, dy, dz]
        from_[axis] = 0
        source = shared
        if any(from_):
            source = tbl.at[pl.ds(row_of(*from_), SEND), :]
        which = code(dx, dy, dz)
        return pltpu.make_async_remote_copy(
            src_ref=source,
            dst_ref=tbl.at[pl.ds(row_of(dx, dy, dz), SEND), :],
            send_sem=fsend_sem.at[which],
            recv_sem=frecv_sem.at[which],
            device_id=device(*go),
            device_id_type=MESH,
        )

    started = []

    def start(copy):
        copy.start()
        started.append(copy)

    for dy in (-1, 1):
        start(halo(0, dy, 0, 1))
    for dx in (-1, 1):
        start(halo(dx, 0, 0, 0))
    for dz in (-1, 1):
        start(halo(0, 0, dz, 2))

    near = nbr_ref[...]
    ghost = near - ATOMS
    block = ghost >> 6
    inside = ghost & 63
    step_x = (block * 57) >> 9
    line = (block * 43) >> 7
    step_y = line - 3 * step_x
    step_z = block - 3 * line
    spot = 3 * step_x + step_y
    flat = FLAT0 + SEND * (spot - jnp.where(spot > 4, 1, 0)) + inside
    paired = PAIR0 + 2 * SEND * spot + jnp.where(step_z > 1, SEND, 0) + inside
    own = near < ATOMS
    index[...] = jnp.where(own, near, jnp.where(step_z == 1, flat, paired))
    shifts = [
        jnp.where(own, 0.0, EDGE * (step - 1).astype(F32)) for step in (step_x, step_y, step_z)
    ]
    for slot in range(SLOTS):
        lanes = slice(128 * slot, 128 * slot + 128)
        base[:, lanes] = (
            jnp.concatenate([each[slot : slot + 1] for each in shifts] + [jnp.zeros((5, ATOMS), F32)], 0)
            - pos8
        )

    rows_iota = lax.broadcasted_iota(jnp.int32, (ATOMS, ATOMS), 0)

    def fill(slot, carry):
        lanes = pl.ds(pl.multiple_of(slot * ATOMS, ATOMS), ATOMS)
        wanted = index[pl.ds(slot, 1), :]
        for part in range(ROWS // ATOMS):
            onehot[part * ATOMS : (part + 1) * ATOMS, lanes] = jnp.where(
                rows_iota == wanted - part * ATOMS, 1.0, 0.0
            ).astype(BF16)
        return carry

    lax.fori_loop(0, SLOTS, fill, 0)

    def flip(row):
        for tile in range(5):
            lanes = slice(128 * tile, 128 * tile + 128)
            tbl_t[lanes, row : row + ATOMS] = dot(
                eye_big, tbl[row : row + ATOMS, lanes], NT
            ).astype(BF16)

    flip(0)

    for dy in (-1, 1):
        halo(0, dy, 0, 1).wait_recv()
        for dx in (-1, 1):
            start(halo(dx, dy, 0, 0))
        for dz in (-1, 1):
            start(halo(0, dy, dz, 2))
    for dy in (0, -1, 1):
        for dx in (-1, 1):
            halo(dx, dy, 0, 0).wait_recv()
            for dz in (-1, 1):
                start(halo(dx, dy, dz, 2))
    for pair in range(4):
        flip(FLAT0 + ATOMS * pair)
    for dx, dy in ((0, 0), (0, -1), (0, 1), (-1, 0), (1, 0), (-1, -1), (1, -1), (-1, 1), (1, 1)):
        for dz in (-1, 1):
            halo(dx, dy, dz, 2).wait_recv()
        flip(row_of(dx, dy, -1))
    for copy in started:
        copy.wait_send()

    def gather(step, carry):
        lanes = pl.ds(pl.multiple_of(step * 256, 256), 256)
        rows = dot(tbl_t[...], onehot[:, lanes])
        gath[:, lanes] = rows[0:FEAT].astype(BF16)
        placed[:, lanes] = rows[FEAT : FEAT + 8] + rows[FEAT + 8 : FEAT + 16] + rows[FEAT + 16 : FEAT + 24]
        return carry

    lax.fori_loop(0, EDGES // 256, gather, 0)

    displace = placed[...] + base[...]
    comp = [displace[axis : axis + 1] for axis in range(3)]
    radius = jnp.sqrt(comp[0] * comp[0] + comp[1] * comp[1] + comp[2] * comp[2] + 1.0)
    inverse = 1.0 / radius
    ux, uy, uz = (each * inverse for each in comp)
    harm[0:8, :] = jnp.concatenate(
        [
            ROOT_THREE * ux,
            ROOT_THREE * uy,
            ROOT_THREE * uz,
            ROOT_FIFTEEN * ux * uy,
            ROOT_FIFTEEN * uy * uz,
            0.5 * ROOT_FIVE * (2.0 * uz * uz - ux * ux - uy * uy),
            ROOT_FIFTEEN * ux * uz,
            0.5 * ROOT_FIFTEEN * (ux * ux - uy * uy),
        ],
        0,
    )
    spacing = radius - 1.25 * lax.broadcasted_iota(jnp.int32, (8, EDGES), 0).astype(F32)
    basis = jnp.exp(-0.5 * spacing * spacing)
    before = dot(rin_ref[...], basis, TN, HIGH)
    pre[...] = before
    hidden = before / (1.0 + jnp.exp(-before))
    radial[...] = dot(rout_ref[...], hidden, TN, HIGH)

    accum[...] = jnp.zeros((FEAT, ATOMS), F32)

    def forward(slot, carry):
        lanes = pl.ds(pl.multiple_of(slot * ATOMS, ATOMS), ATOMS)
        for part in range(4):
            low = 16 * part
            first = gath[low : low + 16, lanes].astype(F32)
            for m in range(9):
                rows = slice(CH * m + low, CH * m + low + 16)
                weight = radial[CH * LEVELS[m] + low : CH * LEVELS[m] + low + 16, lanes]
                if m == 0:
                    value = first + first
                else:
                    value = harm[m - 1 : m, lanes] * first + gath[rows, lanes].astype(F32)
                accum[rows, :] += weight * value
        return carry

    lax.fori_loop(0, SLOTS, forward, 0)

    norm = 1.0 / math.sqrt(SLOTS)
    kinds = (spec_ref[...] == 1).astype(F32)
    sheet = jnp.concatenate([read_ref[0], read_ref[1]], 0)
    level_row = lax.broadcasted_iota(jnp.int32, (6, ATOMS), 0)
    energy = jnp.zeros((1, ATOMS), F32)
    for level in range(3):
        chosen = jnp.where(level_row == level, 1.0 - kinds, 0.0) + jnp.where(
            level_row == level + 3, kinds, 0.0
        )
        weight = dot(sheet, chosen, TN, HIGH)
        total = jnp.zeros((CH, ATOMS), F32)
        for m in range(9):
            if LEVELS[m] != level:
                continue
            rows = slice(CH * m, CH * m + CH)
            value = accum[rows, :] * norm
            if level == 0:
                total = value
                accum[rows, :] = weight * norm
            else:
                total = total + value * value
                accum[rows, :] = (2.0 * norm) * weight * value
        energy = energy + jnp.sum(weight * total, 0, keepdims=True)
    energy_ref[...] = energy

    def backward(slot, carry):
        lanes = pl.ds(pl.multiple_of(slot * ATOMS, ATOMS), ATOMS)
        turns = [None] * 9
        for part in range(4):
            low = 16 * part
            first = gath[low : low + 16, lanes].astype(F32)
            weights = [radial[CH * l + low : CH * l + low + 16, lanes] for l in range(3)]
            slope = accum[low : low + 16, :]
            grad_first = 2.0 * (slope * weights[0])
            grad_radial = [2.0 * (slope * first), None, None]
            for m in range(1, 9):
                level = LEVELS[m]
                rows = slice(CH * m + low, CH * m + low + 16)
                slope = accum[rows, :]
                turn = harm[m - 1 : m, lanes]
                weighted = slope * weights[level]
                high, rest = split(weighted)
                drows[rows, lanes] = high
                dlow[rows, lanes] = rest
                grad_first = grad_first + weighted * turn
                term = slope * (turn * first + gath[rows, lanes].astype(F32))
                grad_radial[level] = term if grad_radial[level] is None else grad_radial[level] + term
                spin = weighted * first
                turns[m] = spin if turns[m] is None else turns[m] + spin
            high, rest = split(grad_first)
            drows[low : low + 16, lanes] = high
            dlow[low : low + 16, lanes] = rest
            for level in range(3):
                drad[CH * level + low : CH * level + low + 16, lanes] = grad_radial[level]
        dharm[:, lanes] = jnp.concatenate(
            [jnp.sum(turns[m], 0, keepdims=True) for m in range(1, 9)], 0
        )
        return carry

    lax.fori_loop(0, SLOTS, backward, 0)

    before = pre[...]
    sigmoid = 1.0 / (1.0 + jnp.exp(-before))
    grad_hidden = dot(rout_ref[...], drad[...], NN, HIGH)
    grad_before = grad_hidden * (sigmoid * (1.0 + before * (1.0 - sigmoid)))
    grad_basis = dot(rin_ref[...], grad_before, NN, HIGH)
    grad_radius = jnp.sum(-(grad_basis * basis * spacing), 0, keepdims=True)
    dy1, dy2, dy3, dy4, dy5, dy6, dy7, dy8 = (dharm[m : m + 1, :] for m in range(8))
    grad_ux = ROOT_THREE * dy1 + ROOT_FIFTEEN * (uy * dy4 + uz * dy7 + ux * dy8) - ROOT_FIVE * ux * dy6
    grad_uy = ROOT_THREE * dy2 + ROOT_FIFTEEN * (ux * dy4 + uz * dy5 - uy * dy8) - ROOT_FIVE * uy * dy6
    grad_uz = ROOT_THREE * dy3 + ROOT_FIFTEEN * (uy * dy5 + ux * dy7) + 2.0 * ROOT_FIVE * uz * dy6
    along = ux * grad_ux + uy * grad_uy + uz * grad_uz
    grad_displace = jnp.concatenate(
        [
            (grad - unit * along) * inverse + grad_radius * unit
            for grad, unit in ((grad_ux, ux), (grad_uy, uy), (grad_uz, uz))
        ]
        + [jnp.zeros((5, EDGES), F32)],
        0,
    )
    drows[FEAT:WIDE, :] = parts(grad_displace)
    dlow[FEAT:WIDE, :] = jnp.zeros((WIDE - FEAT, EDGES), BF16)
    moved = grad_displace[:, 0:ATOMS]
    for slot in range(1, SLOTS):
        moved = moved + grad_displace[:, ATOMS * slot : ATOMS * slot + ATOMS]

    def back(source, target, which, go):
        return pltpu.make_async_remote_copy(
            src_ref=source,
            dst_ref=target,
            send_sem=bsend_sem.at[which],
            recv_sem=brecv_sem.at[which],
            device_id=device(*go),
            device_id_type=MESH,
        )

    def back_z(dx, dy, dz):
        where = pl.ds(row_of(dx, dy, dz) - PAIR0, SEND)
        return back(zsend.at[where, :], zrecv.at[where, :], code(dx, dy, dz), (0, 0, dz))

    def back_x(dx, dy):
        which = 3 * (dx > 0) + dy + 1
        return back(xsend.at[which], xrecv.at[which], code(dx, dy, 0), (dx, 0, 0))

    def back_y(dy):
        which = 1 * (dy > 0)
        return back(ysend.at[which], yrecv.at[which], code(0, dy, 0), (0, dy, 0))

    sent = []

    def send(copy):
        copy.start()
        sent.append(copy)

    for dx in (-1, 1, 0):
        row = row_of(dx, -1, -1)
        zsend[row - PAIR0 : row - PAIR0 + 384, :] = dot(
            onehot[row : row + 384, :], drows[...], NT
        ).astype(BF16)
        for dy in (-1, 1, 0):
            for dz in (-1, 1):
                send(back_z(dx, dy, dz))
    acc0[...] = dot(onehot[0:PAIR0, :], drows[...], NT)
    acc0[0:ATOMS, :] += dot(onehot[0:ATOMS, :], dlow[...], NT)

    def arrived_z(dx, dy):
        total = None
        for dz in (-1, 1):
            back_z(dx, dy, dz).wait_recv()
            row = row_of(dx, dy, dz) - PAIR0
            value = zrecv[row : row + SEND, :].astype(F32)
            total = value if total is None else total + value
        if (dx, dy) == (0, 0):
            return total
        row = row_of(dx, dy, 0)
        return total + acc0[row : row + SEND, :]

    for dy in (-1, 1, 0):
        for dx in (-1, 1):
            xsend[3 * (dx > 0) + dy + 1] = arrived_z(dx, dy).astype(BF16)
            send(back_x(dx, dy))
    totals = []
    for dy in (-1, 1, 0):
        total = arrived_z(0, dy)
        for dx in (-1, 1):
            back_x(dx, dy).wait_recv()
            total = total + xrecv[3 * (dx > 0) + dy + 1].astype(F32)
        if dy:
            ysend[1 * (dy > 0)] = total.astype(BF16)
            send(back_y(dy))
    for dy in (-1, 1):
        back_y(dy).wait_recv()
        total = total + yrecv[1 * (dy > 0)].astype(F32)
    high, rest = split(total)
    owned = acc0[0:ATOMS, :] + dot(picks_t, high) + dot(picks_t, rest)
    for tile in range(4):
        lanes = slice(128 * tile, 128 * tile + 128)
        high, rest = split(owned[:, lanes])
        fgrad_ref[:, lanes] = dot(high, mix[tile], NT) + dot(rest, mix[tile], NT)
    high, rest = split(owned[:, 512:FEAT])
    fgrad_ref[:, 512:FEAT] = dot(high, mix_ref[2], NT) + dot(rest, mix_ref[2], NT)
    turned = dot(eye(SEND).astype(F32), owned[:, FEAT:WIDE], NT, HIGH)
    force = moved - (turned[0:8] + turned[8:16] + turned[16:24])
    force_ref[...] = force[0:3]
    for copy in sent:
        copy.wait_send()


def shards(
    positions, features, species, neighbours, send_list, mix_weight, radial_in, radial_out, readout
):
    vmem = pl.BlockSpec(memory_space=pltpu.VMEM)
    energy, forces, feature_grad = pl.pallas_call(
        kernel,
        out_shape=(
            jax.ShapeDtypeStruct((1, ATOMS), F32),
            jax.ShapeDtypeStruct((3, ATOMS), F32),
            jax.ShapeDtypeStruct((ATOMS, FEAT), F32),
        ),
        in_specs=[vmem] * 9,
        out_specs=(vmem, vmem, vmem),
        scratch_shapes=[
            pltpu.VMEM((ROWS, WIDE), BF16),
            pltpu.VMEM((WIDE, ROWS), BF16),
            pltpu.VMEM((SEND, WIDE), BF16),
            pltpu.VMEM((ROWS, EDGES), BF16),
            pltpu.VMEM((FEAT, EDGES), BF16),
            pltpu.VMEM((8, EDGES), F32),
            pltpu.VMEM((8, EDGES), F32),
            pltpu.VMEM((SLOTS, ATOMS), jnp.int32),
            pltpu.VMEM((3 * CH, EDGES), F32),
            pltpu.VMEM((CH, EDGES), F32),
            pltpu.VMEM((8, EDGES), F32),
            pltpu.VMEM((FEAT, ATOMS), F32),
            pltpu.VMEM((WIDE, EDGES), BF16),
            pltpu.VMEM((WIDE, EDGES), BF16),
            pltpu.VMEM((3 * CH, EDGES), F32),
            pltpu.VMEM((8, EDGES), F32),
            pltpu.VMEM((PAIR0, WIDE), F32),
            pltpu.VMEM((ROWS - PAIR0, WIDE), BF16),
            pltpu.VMEM((ROWS - PAIR0, WIDE), BF16),
            pltpu.VMEM((6, SEND, WIDE), BF16),
            pltpu.VMEM((6, SEND, WIDE), BF16),
            pltpu.VMEM((2, SEND, WIDE), BF16),
            pltpu.VMEM((2, SEND, WIDE), BF16),
            pltpu.SemaphoreType.DMA((27,)),
            pltpu.SemaphoreType.DMA((27,)),
            pltpu.SemaphoreType.DMA((27,)),
            pltpu.SemaphoreType.DMA((27,)),
        ],
        compiler_params=pltpu.CompilerParams(
            collective_id=0, has_side_effects=True, vmem_limit_bytes=60 * 1024 * 1024
        ),
        name="layer",
    )(
        positions[0, 0, 0],
        features[0, 0, 0],
        species[0, 0],
        neighbours[0, 0, 0],
        send_list[0, 0],
        mix_weight,
        radial_in,
        radial_out,
        readout,
    )
    return (energy[None, None], forces[None, None, None], feature_grad[None, None, None])


def solution(mesh):
    in_specs = (
        P("gx", "gy", "gz", None, None),
        P("gx", "gy", "gz", None, None),
        P("gx", "gy", "gz", None),
        P("gx", "gy", "gz", None, None),
        P("gx", "gy", "gz", None),
        P(),
        P(),
        P(),
        P(),
    )
    out_specs = (
        P("gx", "gy", "gz", None),
        P("gx", "gy", "gz", None, None),
        P("gx", "gy", "gz", None, None),
    )
    return jax.shard_map(shards, mesh=mesh, in_specs=in_specs, out_specs=out_specs, check_vma=False)
```

time: 275 us -> 92.9 us (0.34)
  the two profiles are of different devices: /device:TPU:6 before, /device:TPU:1 now
where the time goes in v1:
time: 92.9 us; the launch traced here: 92.7 us
  Pallas kernels  84.3 us (91%)
  local copies, waits for them, and re-layouts  7.75 us (8%)
    pallas_call x1, Pallas kernels, shards(): pl.pallas_call(kernel, out_shape=(jax.ShapeDtypeStruct((1, ATOMS), F32),...  84.3 us
    unnamed x17, local copies, waits for them, and re-layouts  7.75 us

profile of v1, /device:TPU:1, one launch (start us, length us, event | category | flops | bytes accessed | tf_op | source)
XLA Modules:
  0.0 92.7 jit_solution(2926111708854321683)
XLA Ops:
  0.6 0.0 copy-start.3
  0.6 0.0 copy-start.1
  0.7 0.7 copy-done.3
  1.3 0.0 copy-start
  1.3 0.6 copy.21
  1.9 0.0 copy-done.1
  1.9 0.6 copy.13.read_ref
  2.5 0.0 copy-done
  2.5 0.6 copy.20
  3.1 1.7 %copy.12 = bf16[1,1,1,128,576]{4,3,2,1,0:T(8,128)(2,1)} copy(bf16[1,1,1,128,576]{3,4,2,1,0:T(8,128)(2,1)} %param.10) | data formatting | bytes 294912 | tf_op args[1]
  4.8 84.3 %layer.1 = (f32[1,128]{1,0:T(1,128)}, f32[3,128]{1,0:T(4,128)}, f32[128,576]{1,0:T(8,128)}) custom-call(f32[3,128]{1,0:T(4,128)} %bitcast.15, bf16[128,576]{1,0:T(8,128)(2,1)} %bitcast.12, s32[1,128]{1,0:T(1,128)} %bitcast.17, s32[12,128]{1,0:T(8,128)} %bitcast.14, s32[1,64]{1,0:T(1,128)} %bitcast.18, bf16[3,64,64]{2,1,0:T(8,128)(2,1)} %mix_ref.1, ...), custom_call_target="tpu_custom_call" | custom-call | tf_op jit(solution)/shard_map/layer/pallas_call | solution.py:488
  89.1 0.0 copy-start.2
  89.1 0.7 copy-done.2
  89.8 0.6 copy.14
  90.3 0.0 copy-start.4
  90.3 1.8 %copy.15 = f32[1,1,1,128,576]{3,4,2,1,0:T(8,128)} copy(f32[1,1,1,128,576]{4,3,2,1,0:T(8,128)} %bitcast.13) | data formatting | bytes 589824
  92.2 0.0 copy-done.4
  92.2 0.5 copy.23
Async XLA Ops:
  0.6 0.7 copy-start.3
  0.6 1.3 %copy-start.1 = (f32[2,3,64]{2,0,1:T(2,128)S(1)}, f32[2,3,64]{2,0,1:T(2,128)}, u32[]{:S(2)}) copy-start(f32[2,3,64]{2,0,1:T(2,128)} %param.17) | copy-start | bytes 4612
  1.3 1.2 %copy-start = (s32[1,1,1,12,128]{4,2,3,1,0:T(1,128)S(1)}, s32[1,1,1,12,128]{4,2,3,1,0:T(1,128)}, u32[]{:S(2)}) copy-start(s32[1,1,1,12,128]{4,2,3,1,0:T(1,128)} %param.12) | copy-start | bytes 18436
  89.1 0.7 copy-start.2
  90.3 1.8 %copy-start.4 = (f32[1,128]{1,0:T(1,128)S(1)}, f32[1,128]{1,0:T(1,128)}, u32[]{:S(2)}) copy-start(f32[1,128]{1,0:T(1,128)} %get-tuple-element.6) | copy-start | bytes 1540

commit v2 on v1

v2 whole, which is shorter than its diff:
```python
import math

import jax
import jax.numpy as jnp
from jax import lax
from jax.experimental import pallas as pl
from jax.experimental.pallas import tpu as pltpu
from jax.sharding import PartitionSpec as P

EDGE = 3.0
HIGH = lax.Precision.HIGHEST
MESH = pl.DeviceIdType.MESH
LEVELS = (0, 1, 1, 1, 2, 2, 2, 2, 2)
ROOT_THREE = math.sqrt(3.0)
ROOT_FIVE = math.sqrt(5.0)
ROOT_FIFTEEN = math.sqrt(15.0)

ATOMS = 128
SEND = 64
SLOTS = 12
EDGES = SLOTS * ATOMS
CH = 64
FEAT = 576
HALF = 288
RUN = 4

ORDER = ((0, -1), (0, 1), (-1, 0), (1, 0), (-1, -1), (1, -1), (-1, 1), (1, 1))
FLAT0 = 256
PAIR0 = 768
ROWS = 1792
BLOCKS = ROWS // SEND

NN = (((1,), (0,)), ((), ()))
NT = (((1,), (1,)), ((), ()))
TN = (((0,), (0,)), ((), ()))
F32 = jnp.float32
BF16 = jnp.bfloat16


def dot(lhs, rhs, dims=NN, precision=None):
    return lax.dot_general(lhs, rhs, dims, precision=precision, preferred_element_type=F32)


def column(dx, dy):
    return (dx + 1) * 3 + dy + 1


def slot_of(dx, dy, dz):
    if (dx, dy) == (0, 0):
        return 2 + (dz > 0)
    rank = ORDER.index((dx, dy))
    if dz == 0:
        return FLAT0 // SEND + rank
    return PAIR0 // SEND + 2 * rank + (dz > 0)


def parts(value):
    first = value[0:3].astype(BF16).astype(F32)
    rest = value[0:3] - first
    second = rest.astype(BF16).astype(F32)
    filler = jnp.zeros((7, value.shape[1]), F32)
    return jnp.concatenate([first, second, rest - second, filler], 0)


def joined(rows):
    total = rows[0:3] + rows[3:6] + rows[6:9]
    return jnp.concatenate([total, jnp.zeros((5, rows.shape[1]), F32)], 0)


def split(value):
    high = value.astype(BF16)
    return high, (value - high.astype(F32)).astype(BF16)


def mixers(mix_ref):
    zero = jnp.zeros((CH, CH), BF16)

    def pair(upper, lower):
        return jnp.concatenate(
            [
                jnp.concatenate([mix_ref[upper], zero], 1),
                jnp.concatenate([zero, mix_ref[lower]], 1),
            ],
            0,
        )

    last = pair(2, 2)
    return (pair(0, 1), pair(1, 1), last, last)


def kernel(
    pos_ref,
    feat_ref,
    spec_ref,
    nbr_ref,
    list_ref,
    mix_ref,
    rin_ref,
    rout_ref,
    read_ref,
    energy_ref,
    force_ref,
    fgrad_ref,
    shared,
    ghosts,
    place,
    tbl,
    prows,
    onehot,
    inner,
    blocks,
    total_g,
    gath,
    placed,
    base,
    index,
    radial,
    pre,
    harm,
    basis_ref,
    accum,
    drows,
    dlow,
    drad,
    dharm,
    masked,
    own_g,
    flat_g,
    zsend,
    zrecv,
    xsend,
    xrecv,
    ysend,
    yrecv,
    pgrad,
    pzrecv,
    pxsend,
    pxrecv,
    pysend,
    pyrecv,
    fsend_sem,
    frecv_sem,
    bsend_sem,
    brecv_sem,
    psend_sem,
    precv_sem,
):
    size_x, size_y, size_z = (lax.axis_size(name) for name in ("gx", "gy", "gz"))
    me_x, me_y, me_z = (lax.axis_index(name) for name in ("gx", "gy", "gz"))
    run_at = lax.rem(me_x, RUN)
    bend = {-1: -jnp.where(run_at == 0, 1, 0), 1: jnp.where(run_at == RUN - 1, 1, 0)}

    def device(dx, dy, dz):
        turn = bend[dx] if dx else 0
        return (
            lax.rem(me_x + dx + size_x, size_x),
            lax.rem(me_y + dy + turn + size_y, size_y),
            lax.rem(me_z + dz + size_z, size_z),
        )

    sides = ((0, -1, 0), (0, 1, 0), (-1, 0, 0), (1, 0, 0), (0, 0, -1), (0, 0, 1))
    barrier = pltpu.get_barrier_semaphore()
    for side in sides:
        pl.semaphore_signal(barrier, inc=1, device_id=device(*side), device_id_type=MESH)

    mix = mixers(mix_ref)
    pos8 = jnp.concatenate([pos_ref[0], pos_ref[1], pos_ref[2], jnp.zeros((5, ATOMS), F32)], 0)
    for tile in range(4):
        rows = slice(128 * tile, 128 * tile + 128)
        tbl[rows, 0:ATOMS] = dot(mix[tile], feat_ref[rows, :], TN).astype(BF16)
    tbl[512:FEAT, 0:ATOMS] = dot(mix_ref[2], feat_ref[512:FEAT, :], TN).astype(BF16)
    picks = jnp.where(
        lax.broadcasted_iota(jnp.int32, (ATOMS, SEND), 0) == list_ref[...], 1.0, 0.0
    ).astype(BF16)
    zero = jnp.zeros((ATOMS, SEND), BF16)
    picks_left = jnp.concatenate([picks, zero], 1)
    picks_right = jnp.concatenate([zero, picks], 1)
    shared[...] = (
        dot(tbl[0:HALF, 0:ATOMS], picks_left) + dot(tbl[HALF:FEAT, 0:ATOMS], picks_right)
    ).astype(BF16)
    pos_parts = parts(pos8).astype(BF16)
    place[0, 4] = joined(dot(pos_parts, picks_left))

    pl.semaphore_wait(barrier, len(sides))

    started = []

    def start(copy):
        copy.start()
        started.append(copy)

    def remote(source, target, sends, recvs, which, go):
        return pltpu.make_async_remote_copy(
            src_ref=source,
            dst_ref=target,
            send_sem=sends.at[which],
            recv_sem=recvs.at[which],
            device_id=device(*go),
            device_id_type=MESH,
        )

    def halo(dx, dy, dz, axis):
        go = [0, 0, 0]
        go[axis] = -(dx, dy, dz)[axis]
        origin = [dx, dy, dz]
        origin[axis] = 0
        source = ghosts.at[slot_of(*origin)] if any(origin) else shared
        which = slot_of(dx, dy, dz)
        return remote(source, ghosts.at[which], fsend_sem, frecv_sem, which, go)

    def halo_place(axis, side):
        which = 2 * axis + (side > 0)
        if axis == 1:
            source, target, go = place.at[0, 4], place.at[0, 4 + side], (0, -side, 0)
        elif axis == 0:
            source, target = place.at[0, pl.ds(3, 3)], place.at[0, pl.ds(3 + 3 * side, 3)]
            go = (-side, 0, 0)
        else:
            source, target, go = place.at[0], place.at[1 + (side > 0)], (0, 0, -side)
        return remote(source, target, psend_sem, precv_sem, which, go)

    for side in (-1, 1):
        start(halo_place(1, side))
    for dy in (-1, 1):
        start(halo(0, dy, 0, 1))
    for dx in (-1, 1):
        start(halo(dx, 0, 0, 0))
    for dz in (-1, 1):
        start(halo(0, 0, dz, 2))

    near = jnp.concatenate([nbr_ref[slot] for slot in range(SLOTS)], 0)
    ghost = near - ATOMS
    block = ghost >> 6
    step_x = (block * 57) >> 9
    line = (block * 43) >> 7
    step_y = line - 3 * step_x
    step_z = block - 3 * line
    through = step_y - jnp.where(step_x == 0, bend[-1], jnp.where(step_x == 2, bend[1], 0))
    through = jnp.where(through < 0, through + 3, jnp.where(through > 2, through - 3, through))
    spot = 3 * step_x + through
    flat = jnp.zeros_like(spot)
    paired = jnp.full_like(spot, ATOMS)
    for rank, (dx, dy) in enumerate(ORDER):
        here = spot == column(dx, dy)
        flat = jnp.where(here, FLAT0 + SEND * rank, flat)
        paired = jnp.where(here, PAIR0 + 2 * SEND * rank, paired)
    paired = paired + jnp.where(step_z > 1, SEND, 0)
    own = near < ATOMS
    row = jnp.where(own, near, jnp.where(step_z == 1, flat, paired) + (ghost & 63))
    index[...] = row
    shifts = [
        jnp.where(own, 0.0, EDGE * (step - 1).astype(F32)) for step in (step_x, step_y, step_z)
    ]
    for slot in range(SLOTS):
        lanes = slice(128 * slot, 128 * slot + 128)
        blocks[0:1, lanes] = row[slot : slot + 1] >> 6
        base[:, lanes] = (
            jnp.concatenate([each[slot : slot + 1] for each in shifts] + [jnp.zeros((5, ATOMS), F32)], 0)
            - pos8
        )

    rows_iota = lax.broadcasted_iota(jnp.int32, (ATOMS, ATOMS), 0)

    def fill(slot, carry):
        lanes = pl.ds(pl.multiple_of(slot * ATOMS, ATOMS), ATOMS)
        wanted = index[pl.ds(slot, 1), :]
        inner[:, lanes] = jnp.where(rows_iota[0:SEND] == (wanted & 63), 1.0, 0.0).astype(BF16)
        for part in range(ROWS // ATOMS):
            onehot[part * ATOMS : (part + 1) * ATOMS, lanes] = jnp.where(
                rows_iota == wanted - part * ATOMS, 1.0, 0.0
            ).astype(BF16)
        return carry

    lax.fori_loop(0, SLOTS, fill, 0)

    def settle(row, left, right):
        lanes = slice(row, row + 128)
        for part in range(2):
            half = slice(SEND * part, SEND * part + SEND)
            tbl[HALF * part : HALF * part + HALF, lanes] = jnp.concatenate(
                [ghosts[left][:, half], ghosts[right][:, half]], 1
            )

    def settle_pair(dx, dy):
        left, right = slot_of(dx, dy, -1), slot_of(dx, dy, 1)
        settle(SEND * left, left, right)

    def gather(low, high):
        def one(step, carry):
            lanes = pl.ds(pl.multiple_of(step * 256, 256), 256)
            rows = dot(tbl[:, low:high], onehot[low:high, lanes])
            if low:
                rows = rows + total_g[:, lanes]
            if high == ROWS:
                gath[:, lanes] = rows.astype(BF16)
            else:
                total_g[:, lanes] = rows
            return carry

        lax.fori_loop(0, EDGES // 256, one, 0)

    for side in (-1, 1):
        halo_place(1, side).wait_recv()
    for side in (-1, 1):
        start(halo_place(0, side))
    for dy in (-1, 1):
        halo(0, dy, 0, 1).wait_recv()
        for dx in (-1, 1):
            start(halo(dx, dy, 0, 0))
        for dz in (-1, 1):
            start(halo(0, dy, dz, 2))
    for side in (-1, 1):
        halo_place(0, side).wait_recv()
    for side in (-1, 1):
        start(halo_place(2, side))
    for dx in (-1, 1):
        halo(dx, 0, 0, 0).wait_recv()
        for dz in (-1, 1):
            start(halo(dx, 0, dz, 2))
    for dz in (-1, 1):
        halo(0, 0, dz, 2).wait_recv()
    settle_pair(0, 0)
    gather(0, FLAT0)
    for dy in (-1, 1):
        for dx in (-1, 1):
            halo(dx, dy, 0, 0).wait_recv()
            for dz in (-1, 1):
                start(halo(dx, dy, dz, 2))
    for rank in range(0, 8, 2):
        left = FLAT0 // SEND + rank
        settle(SEND * left, left, left + 1)
    gather(FLAT0, PAIR0)

    for side in (-1, 1):
        halo_place(2, side).wait_recv()
    for half in range(2):
        prows[16 * half : 16 * half + 16, 0:SEND] = pos_parts[:, SEND * half : SEND * half + SEND]
    for dx in (-1, 0, 1):
        for dy in (-1, 0, 1):
            for dz in (-1, 0, 1):
                if (dx, dy, dz) != (0, 0, 0):
                    slot = slot_of(dx, dy, dz)
                    prows[16 * slot : 16 * slot + 16, :] = parts(
                        place[0 if dz == 0 else 1 + (dz > 0), column(dx, dy)]
                    ).astype(BF16)

    def locate(step, carry):
        lanes = pl.ds(pl.multiple_of(step * 256, 256), 256)
        rows = dot(prows[:, 0:SEND], inner[:, lanes])
        where = blocks[0:1, lanes]
        chosen = jnp.zeros((16, 256), F32)
        for slot in range(BLOCKS):
            chosen = jnp.where(where == slot, rows[16 * slot : 16 * slot + 16], chosen)
        placed[:, lanes] = joined(chosen)
        return carry

    lax.fori_loop(0, EDGES // 256, locate, 0)
    displace = placed[...] + base[...]
    comp = [displace[axis : axis + 1] for axis in range(3)]
    radius = jnp.sqrt(comp[0] * comp[0] + comp[1] * comp[1] + comp[2] * comp[2] + 1.0)
    inverse = 1.0 / radius
    ux, uy, uz = (each * inverse for each in comp)
    harm[0:8, :] = jnp.concatenate(
        [
            ROOT_THREE * ux,
            ROOT_THREE * uy,
            ROOT_THREE * uz,
            ROOT_FIFTEEN * ux * uy,
            ROOT_FIFTEEN * uy * uz,
            0.5 * ROOT_FIVE * (2.0 * uz * uz - ux * ux - uy * uy),
            ROOT_FIFTEEN * ux * uz,
            0.5 * ROOT_FIFTEEN * (ux * ux - uy * uy),
        ],
        0,
    )
    spacing = radius - 1.25 * lax.broadcasted_iota(jnp.int32, (8, EDGES), 0).astype(F32)
    basis = jnp.exp(-0.5 * spacing * spacing)
    basis_ref[...] = basis * spacing
    before = dot(rin_ref[...], basis, TN, HIGH)
    pre[...] = before
    hidden = before / (1.0 + jnp.exp(-before))
    radial[...] = dot(rout_ref[...], hidden, TN, HIGH)

    for dx, dy in ORDER[:4]:
        for dz in (-1, 1):
            halo(dx, dy, dz, 2).wait_recv()
        settle_pair(dx, dy)
    gather(PAIR0, PAIR0 + 512)
    for dx, dy in ORDER[4:]:
        for dz in (-1, 1):
            halo(dx, dy, dz, 2).wait_recv()
        settle_pair(dx, dy)
    gather(PAIR0 + 512, ROWS)

    accum[...] = jnp.zeros((FEAT, ATOMS), F32)

    def forward(slot, carry):
        lanes = pl.ds(pl.multiple_of(slot * ATOMS, ATOMS), ATOMS)
        for part in range(4):
            low = 16 * part
            first = gath[low : low + 16, lanes].astype(F32)
            for m in range(9):
                rows = slice(CH * m + low, CH * m + low + 16)
                weight = radial[CH * LEVELS[m] + low : CH * LEVELS[m] + low + 16, lanes]
                if m == 0:
                    value = first + first
                else:
                    value = harm[m - 1 : m, lanes] * first + gath[rows, lanes].astype(F32)
                accum[rows, :] += weight * value
        return carry

    lax.fori_loop(0, SLOTS, forward, 0)

    norm = 1.0 / math.sqrt(SLOTS)
    kinds = (spec_ref[...] == 1).astype(F32)
    by_kind = jnp.concatenate([1.0 - kinds, kinds], 0)
    energy = jnp.zeros((1, ATOMS), F32)
    for level in range(3):
        weight = dot(read_ref[level], by_kind, TN, HIGH)
        total = jnp.zeros((CH, ATOMS), F32)
        for m in range(9):
            if LEVELS[m] != level:
                continue
            rows = slice(CH * m, CH * m + CH)
            value = accum[rows, :] * norm
            if level == 0:
                total = value
                accum[rows, :] = weight * norm
            else:
                total = total + value * value
                accum[rows, :] = (2.0 * norm) * weight * value
        energy = energy + jnp.sum(weight * total, 0, keepdims=True)
    energy_ref[...] = energy

    def backward(slot, carry):
        lanes = pl.ds(pl.multiple_of(slot * ATOMS, ATOMS), ATOMS)
        turns = [None] * 9
        for part in range(4):
            low = 16 * part
            first = gath[low : low + 16, lanes].astype(F32)
            weights = [radial[CH * l + low : CH * l + low + 16, lanes] for l in range(3)]
            slope = accum[low : low + 16, :]
            grad_first = 2.0 * (slope * weights[0])
            grad_radial = [2.0 * (slope * first), None, None]
            for m in range(1, 9):
                level = LEVELS[m]
                rows = slice(CH * m + low, CH * m + low + 16)
                slope = accum[rows, :]
                turn = harm[m - 1 : m, lanes]
                weighted = slope * weights[level]
                high, rest = split(weighted)
                drows[rows, lanes] = high
                dlow[rows, lanes] = rest
                grad_first = grad_first + weighted * turn
                term = slope * (turn * first + gath[rows, lanes].astype(F32))
                grad_radial[level] = term if grad_radial[level] is None else grad_radial[level] + term
                spin = weighted * first
                turns[m] = spin if turns[m] is None else turns[m] + spin
            high, rest = split(grad_first)
            drows[low : low + 16, lanes] = high
            dlow[low : low + 16, lanes] = rest
            for level in range(3):
                drad[CH * level + low : CH * level + low + 16, lanes] = grad_radial[level]
        dharm[:, lanes] = jnp.concatenate(
            [jnp.sum(turns[m], 0, keepdims=True) for m in range(1, 9)], 0
        )
        return carry

    lax.fori_loop(0, SLOTS, backward, 0)

    def back_z(dx, dy, dz):
        which = slot_of(dx, dy, dz) - (2 if (dx, dy) == (0, 0) else PAIR0 // SEND - 2)
        return remote(
            zsend.at[which], zrecv.at[which], bsend_sem, brecv_sem, slot_of(dx, dy, dz), (0, 0, dz)
        )

    def back_x(dx, dy):
        which = 3 * (dx > 0) + dy + 1
        return remote(
            xsend.at[which], xrecv.at[which], bsend_sem, brecv_sem, slot_of(dx, dy, 0), (dx, 0, 0)
        )

    def back_y(dy):
        which = 1 * (dy > 0)
        return remote(
            ysend.at[which], yrecv.at[which], bsend_sem, brecv_sem, slot_of(0, dy, 0), (0, dy, 0)
        )

    def back_place(axis, side):
        at = 1 * (side > 0)
        if axis == 2:
            source, target, go = pgrad.at[1 + at], pzrecv.at[at], (0, 0, side)
        elif axis == 0:
            source, target, go = pxsend.at[at], pxrecv.at[at], (side, 0, 0)
        else:
            source, target, go = pysend.at[at], pyrecv.at[at], (0, side, 0)
        return remote(source, target, psend_sem, precv_sem, 6 + 2 * axis + at, go)

    def folded(pair):
        return [
            jnp.concatenate(
                [pair[0:HALF, SEND * part : SEND * part + SEND], pair[HALF:FEAT, SEND * part : SEND * part + SEND]],
                1,
            )
            for part in range(2)
        ]

    def send_pairs(row, columns):
        rows = dot(drows[...], onehot[row : row + 128 * len(columns), :], NT)
        for at, (dx, dy) in enumerate(columns):
            blocks_ = folded(rows[:, 128 * at : 128 * at + 128])
            for dz, value in zip((-1, 1), blocks_):
                which = slot_of(dx, dy, dz) - (2 if (dx, dy) == (0, 0) else PAIR0 // SEND - 2)
                zsend[which] = value.astype(BF16)
                start(back_z(dx, dy, dz))

    def keep_flats(rank):
        rows = dot(drows[...], onehot[FLAT0 + SEND * rank : FLAT0 + SEND * rank + 256, :], NT)
        for at in range(2):
            for part, value in enumerate(folded(rows[:, 128 * at : 128 * at + 128])):
                flat_g[rank + 2 * at + part] = value

    for rank in (4, 6, 2):
        send_pairs(PAIR0 + 128 * rank, ORDER[rank : rank + 2])

    before = pre[...]
    sigmoid = 1.0 / (1.0 + jnp.exp(-before))
    grad_hidden = dot(rout_ref[...], drad[...], NN, HIGH)
    grad_before = grad_hidden * (sigmoid * (1.0 + before * (1.0 - sigmoid)))
    grad_basis = dot(rin_ref[...], grad_before, NN, HIGH)
    grad_radius = jnp.sum(-(grad_basis * basis_ref[...]), 0, keepdims=True)
    displace = placed[...] + base[...]
    comp = [displace[axis : axis + 1] for axis in range(3)]
    radius = jnp.sqrt(comp[0] * comp[0] + comp[1] * comp[1] + comp[2] * comp[2] + 1.0)
    inverse = 1.0 / radius
    ux, uy, uz = (each * inverse for each in comp)
    dy1, dy2, dy3, dy4, dy5, dy6, dy7, dy8 = (dharm[m : m + 1, :] for m in range(8))
    grad_ux = ROOT_THREE * dy1 + ROOT_FIFTEEN * (uy * dy4 + uz * dy7 + ux * dy8) - ROOT_FIVE * ux * dy6
    grad_uy = ROOT_THREE * dy2 + ROOT_FIFTEEN * (ux * dy4 + uz * dy5 - uy * dy8) - ROOT_FIVE * uy * dy6
    grad_uz = ROOT_THREE * dy3 + ROOT_FIFTEEN * (uy * dy5 + ux * dy7) + 2.0 * ROOT_FIVE * uz * dy6
    along = ux * grad_ux + uy * grad_uy + uz * grad_uz
    grad_displace = jnp.concatenate(
        [
            (grad - unit * along) * inverse + grad_radius * unit
            for grad, unit in ((grad_ux, ux), (grad_uy, uy), (grad_uz, uz))
        ],
        0,
    )
    moved = grad_displace[:, 0:ATOMS]
    for slot in range(1, SLOTS):
        moved = moved + grad_displace[:, ATOMS * slot : ATOMS * slot + ATOMS]
    pieces = parts(grad_displace)
    where = blocks[0:1, :]
    for slot in range(BLOCKS):
        masked[16 * slot : 16 * slot + 16, :] = jnp.where(where == slot, pieces, 0.0).astype(BF16)
    drawn = dot(masked[...], inner[...], NT)
    own_place = joined(jnp.concatenate([drawn[0:16], drawn[16:32]], 1))
    blank = jnp.zeros((8, SEND), F32)
    pgrad[0, 4] = jnp.zeros((8, ATOMS), F32)
    for dx in (-1, 0, 1):
        for dy in (-1, 0, 1):
            for dz in (-1, 0, 1):
                if (dx, dy, dz) != (0, 0, 0):
                    slot = slot_of(dx, dy, dz)
                    pgrad[0 if dz == 0 else 1 + (dz > 0), column(dx, dy)] = jnp.concatenate(
                        [joined(drawn[16 * slot : 16 * slot + 16]), blank], 1
                    )
    for side in (-1, 1):
        start(back_place(2, side))

    for rank in (4, 0):
        keep_flats(rank)
    send_pairs(PAIR0, ORDER[0:2])

    def arrived_z(dx, dy):
        total = None
        for dz in (-1, 1):
            back_z(dx, dy, dz).wait_recv()
            which = slot_of(dx, dy, dz) - (2 if (dx, dy) == (0, 0) else PAIR0 // SEND - 2)
            value = zrecv[which].astype(F32)
            total = value if total is None else total + value
        if (dx, dy) == (0, 0):
            return total
        return total + flat_g[ORDER.index((dx, dy))]

    for dx, dy in (ORDER[4:] + ORDER[2:4]):
        xsend[3 * (dx > 0) + dy + 1] = arrived_z(dx, dy).astype(BF16)
        start(back_x(dx, dy))
    for side in (-1, 1):
        back_place(2, side).wait_recv()
    for side in (-1, 1):
        lines = pl.ds(3 + 3 * side, 3)
        pxsend[1 * (side > 0)] = pgrad[0, lines] + pzrecv[0, lines] + pzrecv[1, lines]
        start(back_place(0, side))

    rows = dot(drows[...], onehot[0:FLAT0, :], NT)
    own_g[...] = rows[:, 0:ATOMS] + dot(dlow[...], onehot[0:ATOMS, :], NT)
    for dz, value in zip((-1, 1), folded(rows[:, ATOMS:FLAT0])):
        zsend[1 * (dz > 0)] = value.astype(BF16)
        start(back_z(0, 0, dz))

    for dy in (-1, 1, 0):
        total = arrived_z(0, dy)
        for dx in (-1, 1):
            back_x(dx, dy).wait_recv()
            total = total + xrecv[3 * (dx > 0) + dy + 1].astype(F32)
        if dy:
            ysend[1 * (dy > 0)] = total.astype(BF16)
            start(back_y(dy))
        if dy == 1:
            for side in (-1, 1):
                back_place(0, side).wait_recv()
            middle = pl.ds(3, 3)
            totals = pgrad[0, middle]
            totals = totals + pzrecv[0, middle] + pzrecv[1, middle] + pxrecv[0] + pxrecv[1]
            pysend[0] = totals[0]
            pysend[1] = totals[2]
            for side in (-1, 1):
                start(back_place(1, side))
    for dy in (-1, 1):
        back_y(dy).wait_recv()
        total = total + yrecv[1 * (dy > 0)].astype(F32)
    high, rest = split(total)
    for part, chosen in enumerate((picks_left, picks_right)):
        rows = slice(HALF * part, HALF * part + HALF)
        own_g[rows, :] += dot(high, chosen, NT) + dot(rest, chosen, NT)
    for tile in range(4):
        rows = slice(128 * tile, 128 * tile + 128)
        high, rest = split(own_g[rows, :])
        fgrad_ref[rows, :] = dot(mix[tile], high) + dot(mix[tile], rest)
    high, rest = split(own_g[512:FEAT, :])
    fgrad_ref[512:FEAT, :] = dot(mix_ref[2], high) + dot(mix_ref[2], rest)

    back = totals[1]
    for side in (-1, 1):
        back_place(1, side).wait_recv()
        back = back + pyrecv[1 * (side > 0)]
    force = moved - own_place[0:3] - joined(dot(parts(back).astype(BF16), picks_left, NT))[0:3]
    for axis in range(3):
        force_ref[axis] = force[axis : axis + 1]
    for copy in started:
        copy.wait_send()


def shards(
    positions, features, species, neighbours, send_list, mix_weight, radial_in, radial_out, readout
):
    vmem = pl.BlockSpec(memory_space=pltpu.VMEM)
    energy, forces, feature_grad = pl.pallas_call(
        kernel,
        out_shape=(
            jax.ShapeDtypeStruct((1, ATOMS), F32),
            jax.ShapeDtypeStruct((3, 1, ATOMS), F32),
            jax.ShapeDtypeStruct((FEAT, ATOMS), F32),
        ),
        in_specs=[vmem] * 9,
        out_specs=(vmem, vmem, vmem),
        scratch_shapes=[
            pltpu.VMEM((HALF, 128), BF16),
            pltpu.VMEM((BLOCKS, HALF, 128), BF16),
            pltpu.VMEM((3, 9, 8, 128), F32),
            pltpu.VMEM((FEAT, ROWS), BF16),
            pltpu.VMEM((16 * BLOCKS, 128), BF16),
            pltpu.VMEM((ROWS, EDGES), BF16),
            pltpu.VMEM((SEND, EDGES), BF16),
            pltpu.VMEM((8, EDGES), jnp.int32),
            pltpu.VMEM((FEAT, EDGES), F32),
            pltpu.VMEM((FEAT, EDGES), BF16),
            pltpu.VMEM((8, EDGES), F32),
            pltpu.VMEM((8, EDGES), F32),
            pltpu.VMEM((SLOTS, ATOMS), jnp.int32),
            pltpu.VMEM((3 * CH, EDGES), F32),
            pltpu.VMEM((CH, EDGES), F32),
            pltpu.VMEM((8, EDGES), F32),
            pltpu.VMEM((8, EDGES), F32),
            pltpu.VMEM((FEAT, ATOMS), F32),
            pltpu.VMEM((FEAT, EDGES), BF16),
            pltpu.VMEM((FEAT, EDGES), BF16),
            pltpu.VMEM((3 * CH, EDGES), F32),
            pltpu.VMEM((8, EDGES), F32),
            pltpu.VMEM((16 * BLOCKS, EDGES), BF16),
            pltpu.VMEM((FEAT, ATOMS), F32),
            pltpu.VMEM((8, HALF, 128), F32),
            pltpu.VMEM((18, HALF, 128), BF16),
            pltpu.VMEM((18, HALF, 128), BF16),
            pltpu.VMEM((6, HALF, 128), BF16),
            pltpu.VMEM((6, HALF, 128), BF16),
            pltpu.VMEM((2, HALF, 128), BF16),
            pltpu.VMEM((2, HALF, 128), BF16),
            pltpu.VMEM((3, 9, 8, 128), F32),
            pltpu.VMEM((2, 9, 8, 128), F32),
            pltpu.VMEM((2, 3, 8, 128), F32),
            pltpu.VMEM((2, 3, 8, 128), F32),
            pltpu.VMEM((2, 8, 128), F32),
            pltpu.VMEM((2, 8, 128), F32),
            pltpu.SemaphoreType.DMA((BLOCKS,)),
            pltpu.SemaphoreType.DMA((BLOCKS,)),
            pltpu.SemaphoreType.DMA((BLOCKS,)),
            pltpu.SemaphoreType.DMA((BLOCKS,)),
            pltpu.SemaphoreType.DMA((12,)),
            pltpu.SemaphoreType.DMA((12,)),
        ],
        compiler_params=pltpu.CompilerParams(
            collective_id=0, has_side_effects=True, vmem_limit_bytes=60 * 1024 * 1024
        ),
        name="layer",
    )(
        positions.reshape(3, 1, ATOMS),
        features[0, 0, 0].T,
        species[0, 0],
        neighbours.reshape(SLOTS, 1, ATOMS),
        send_list[0, 0],
        mix_weight,
        radial_in,
        radial_out,
        jnp.transpose(readout, (1, 0, 2)),
    )
    return (
        energy[None, None],
        forces.reshape(1, 1, 1, 3, ATOMS),
        feature_grad.T[None, None, None],
    )


def solution(mesh):
    in_specs = (
        P("gx", "gy", "gz", None, None),
        P("gx", "gy", "gz", None, None),
        P("gx", "gy", "gz", None),
        P("gx", "gy", "gz", None, None),
        P("gx", "gy", "gz", None),
        P(),
        P(),
        P(),
        P(),
    )
    out_specs = (
        P("gx", "gy", "gz", None),
        P("gx", "gy", "gz", None, None),
        P("gx", "gy", "gz", None, None),
    )
    return jax.shard_map(shards, mesh=mesh, in_specs=in_specs, out_specs=out_specs, check_vma=False)
```

time: 92.9 us -> 75.3 us (0.81)
  the two profiles are of different devices: /device:TPU:1 before, /device:TPU:6 now
where the time goes in v2:
time: 75.3 us; the launch traced here: 75.1 us
  Pallas kernels  71.1 us (94%)
  local copies, waits for them, and re-layouts  3.36 us (4%)
    pallas_call x1, Pallas kernels, shards(): pl.pallas_call(kernel, out_shape=(jax.ShapeDtypeStruct((1, ATOMS), F32),...  71.1 us
    unnamed x7, local copies, waits for them, and re-layouts  3.36 us

profile of v2, /device:TPU:6, one launch (start us, length us, event | category | flops | bytes accessed | tf_op | source)
XLA Modules:
  0.0 75.1 jit_solution(18200676851844910794)
XLA Ops:
  0.6 71.1 %layer.1 = (f32[1,128]{1,0:T(1,128)}, f32[3,1,128]{2,1,0:T(1,128)}, f32[576,128]{1,0:T(8,128)}) custom-call(f32[3,1,128]{2,1,0:T(1,128)} %bitcast.19, bf16[576,128]{1,0:T(8,128)(2,1)} %bitcast.16, s32[1,128]{1,0:T(1,128)} %bitcast.21, s32[12,1,128]{2,1,0:T(1,128)} %bitcast.17, s32[1,64]{1,0:T(1,128)} %bitcast.22, bf16[3,64,64]{2,1,0:T(8,128)(2,1)} %mix_ref.1, ...), custom_call_target="tpu_custom_call" | custom-call | tf_op jit(solution)/shard_map/layer/pallas_call | solution.py:649
  71.7 0.0 copy-start.1
  71.8 0.0 copy-start
  71.8 0.6 copy-done.1
  72.4 0.5 copy.16
  72.9 0.0 copy-done
  72.9 0.6 copy.17
  73.4 1.7 %copy.18 = f32[1,1,1,128,576]{3,4,2,1,0:T(8,128)} copy(f32[1,1,1,128,576]{3,4,2,1,0:T(8,128)} %bitcast.15) | data formatting | bytes 589824
Async XLA Ops:
  71.7 0.6 copy-start.1
  71.8 1.1 %copy-start = (f32[3,1,128]{2,1,0:T(1,128)S(1)}, f32[3,1,128]{2,1,0:T(1,128)}, u32[]{:S(2)}) copy-start(f32[3,1,128]{2,1,0:T(1,128)} %get-tuple-element.7) | copy-start | bytes 4612

commit v3 on v2

--- a/solution.py
+++ b/solution.py
@@ -22,6 +22,8 @@
 CH = 64
 FEAT = 576
 HALF = 288
+CHUNKS = 3
+PIECE = HALF // CHUNKS
 RUN = 4
 
 ORDER = ((0, -1), (0, 1), (-1, 0), (1, 0), (-1, -1), (1, -1), (-1, 1), (1, 1))
@@ -89,62 +91,67 @@
 
 
 def kernel(
-    pos_ref,
-    feat_ref,
-    spec_ref,
-    nbr_ref,
-    list_ref,
-    mix_ref,
-    rin_ref,
-    rout_ref,
-    read_ref,
-    energy_ref,
-    force_ref,
-    fgrad_ref,
-    shared,
-    ghosts,
-    place,
-    tbl,
-    prows,
-    onehot,
-    inner,
-    blocks,
-    total_g,
-    gath,
-    placed,
-    base,
-    index,
-    radial,
-    pre,
-    harm,
-    basis_ref,
-    accum,
-    drows,
-    dlow,
-    drad,
-    dharm,
-    masked,
-    own_g,
-    flat_g,
-    zsend,
-    zrecv,
-    xsend,
-    xrecv,
-    ysend,
-    yrecv,
-    pgrad,
-    pzrecv,
-    pxsend,
-    pxrecv,
-    pysend,
-    pyrecv,
-    fsend_sem,
-    frecv_sem,
-    bsend_sem,
-    brecv_sem,
-    psend_sem,
-    precv_sem,
+    *refs,
 ):
+    arguments, refs = refs[:9], refs[9:]
+    (
+        energy_ref,
+        force_ref,
+        owned_ref,
+        pos_ref,
+        feat_ref,
+        spec_ref,
+        nbr_ref,
+        list_ref,
+        mix_ref,
+        rin_ref,
+        rout_ref,
+        read_ref,
+        shared,
+        ghosts,
+        place,
+        tbl,
+        prows,
+        onehot,
+        inner,
+        blocks,
+        total_g,
+        gath,
+        placed,
+        base,
+        index,
+        radial,
+        pre,
+        harm,
+        basis_ref,
+        accum,
+        drows,
+        dlow,
+        drad,
+        dharm,
+        masked,
+        own_g,
+        flat_g,
+        zsend,
+        zrecv,
+        xsend,
+        xrecv,
+        ysend,
+        yrecv,
+        pgrad,
+        pzrecv,
+        pxsend,
+        pxrecv,
+        pysend,
+        pyrecv,
+        fsend_sem,
+        frecv_sem,
+        bsend_sem,
+        brecv_sem,
+        psend_sem,
+        precv_sem,
+        load_sem,
+    ) = refs
     size_x, size_y, size_z = (lax.axis_size(name) for name in ("gx", "gy", "gz"))
     me_x, me_y, me_z = (lax.axis_index(name) for name in ("gx", "gy", "gz"))
     run_at = lax.rem(me_x, RUN)
@@ -162,6 +169,16 @@
     barrier = pltpu.get_barrier_semaphore()
     for side in sides:
         pl.semaphore_signal(barrier, inc=1, device_id=device(*side), device_id_type=MESH)
+
+    inputs = (pos_ref, feat_ref, spec_ref, nbr_ref, list_ref, mix_ref, rin_ref, rout_ref, read_ref)
+    loads = [
+        pltpu.make_async_copy(source, target, load_sem.at[which])
+        for which, (source, target) in enumerate(zip(arguments, inputs))
+    ]
+    for load in loads:
+        load.start()
+    for load in loads:
+        load.wait()
 
     mix = mixers(mix_ref)
     pos8 = jnp.concatenate([pos_ref[0], pos_ref[1], pos_ref[2], jnp.zeros((5, ATOMS), F32)], 0)
@@ -199,14 +216,23 @@
             device_id_type=MESH,
         )
 
-    def halo(dx, dy, dz, axis):
+    def piece(chunk):
+        return pl.ds(PIECE * chunk, PIECE)
+
+    def halo(dx, dy, dz, axis, chunk):
         go = [0, 0, 0]
         go[axis] = -(dx, dy, dz)[axis]
         origin = [dx, dy, dz]
         origin[axis] = 0
-        source = ghosts.at[slot_of(*origin)] if any(origin) else shared
-        which = slot_of(dx, dy, dz)
-        return remote(source, ghosts.at[which], fsend_sem, frecv_sem, which, go)
+        part = piece(chunk)
+        source = ghosts.at[slot_of(*origin), part] if any(origin) else shared.at[part]
+        slot = slot_of(dx, dy, dz)
+        target = ghosts.at[slot, part]
+        return remote(source, target, fsend_sem, frecv_sem, CHUNKS * slot + chunk, go)
+
+    def wait_halo(dx, dy, dz, axis):
+        for chunk in range(CHUNKS):
+            halo(dx, dy, dz, axis, chunk).wait_recv()
 
     def halo_place(axis, side):
         which = 2 * axis + (side > 0)
@@ -221,12 +247,15 @@
 
     for side in (-1, 1):
         start(halo_place(1, side))
-    for dy in (-1, 1):
-        start(halo(0, dy, 0, 1))
-    for dx in (-1, 1):
-        start(halo(dx, 0, 0, 0))
-    for dz in (-1, 1):
-        start(halo(0, 0, dz, 2))
+    for chunk in range(CHUNKS):
+        for dy in (-1, 1):
+            start(halo(0, dy, 0, 1, chunk))
+    for chunk in range(CHUNKS):
+        for dx in (-1, 1):
+            start(halo(dx, 0, 0, 0, chunk))
+    for chunk in range(CHUNKS):
+        for dz in (-1, 1):
+            start(halo(0, 0, dz, 2, chunk))
 
     near = jnp.concatenate([nbr_ref[slot] for slot in range(SLOTS)], 0)
     ghost = near - ATOMS
@@ -303,29 +332,36 @@
         halo_place(1, side).wait_recv()
     for side in (-1, 1):
         start(halo_place(0, side))
-    for dy in (-1, 1):
-        halo(0, dy, 0, 1).wait_recv()
+    def pass_x(dy, chunk):
+        halo(0, dy, 0, 1, chunk).wait_recv()
         for dx in (-1, 1):
-            start(halo(dx, dy, 0, 0))
+            start(halo(dx, dy, 0, 0, chunk))
         for dz in (-1, 1):
-            start(halo(0, dy, dz, 2))
+            start(halo(0, dy, dz, 2, chunk))
+
+    def pass_z(dx, dy, chunk):
+        halo(dx, dy, 0, 0, chunk).wait_recv()
+        for dz in (-1, 1):
+            start(halo(dx, dy, dz, 2, chunk))
+
+    for chunk in range(CHUNKS):
+        for dy in (-1, 1):
+            pass_x(dy, chunk)
     for side in (-1, 1):
         halo_place(0, side).wait_recv()
     for side in (-1, 1):
         start(halo_place(2, side))
-    for dx in (-1, 1):
-        halo(dx, 0, 0, 0).wait_recv()
-        for dz in (-1, 1):
-            start(halo(dx, 0, dz, 2))
+    for chunk in range(CHUNKS):
+        for dx in (-1, 1):
+            pass_z(dx, 0, chunk)
     for dz in (-1, 1):
-        halo(0, 0, dz, 2).wait_recv()
+        wait_halo(0, 0, dz, 2)
     settle_pair(0, 0)
     gather(0, FLAT0)
-    for dy in (-1, 1):
-        for dx in (-1, 1):
-            halo(dx, dy, 0, 0).wait_recv()
-            for dz in (-1, 1):
-                start(halo(dx, dy, dz, 2))
+    for chunk in range(CHUNKS):
+        for dy in (-1, 1):
+            for dx in (-1, 1):
+                pass_z(dx, dy, chunk)
     for rank in range(0, 8, 2):
         left = FLAT0 // SEND + rank
         settle(SEND * left, left, left + 1)
@@ -383,12 +419,12 @@
 
     for dx, dy in ORDER[:4]:
         for dz in (-1, 1):
-            halo(dx, dy, dz, 2).wait_recv()
+            wait_halo(dx, dy, dz, 2)
         settle_pair(dx, dy)
     gather(PAIR0, PAIR0 + 512)
     for dx, dy in ORDER[4:]:
         for dz in (-1, 1):
-            halo(dx, dy, dz, 2).wait_recv()
+            wait_halo(dx, dy, dz, 2)
         settle_pair(dx, dy)
     gather(PAIR0 + 512, ROWS)
 
@@ -468,23 +504,32 @@
 
     lax.fori_loop(0, SLOTS, backward, 0)
 
-    def back_z(dx, dy, dz):
-        which = slot_of(dx, dy, dz) - (2 if (dx, dy) == (0, 0) else PAIR0 // SEND - 2)
+    def lane_z(dx, dy, dz):
+        return slot_of(dx, dy, dz) - (2 if (dx, dy) == (0, 0) else PAIR0 // SEND - 2)
+
+    def lane_x(dx, dy):
+        return 3 * (dx > 0) + dy + 1
+
+    def back(sends, recvs, lane, slot, chunk, go):
+        part = piece(chunk)
         return remote(
-            zsend.at[which], zrecv.at[which], bsend_sem, brecv_sem, slot_of(dx, dy, dz), (0, 0, dz)
+            sends.at[lane, part],
+            recvs.at[lane, part],
+            bsend_sem,
+            brecv_sem,
+            CHUNKS * slot + chunk,
+            go,
         )
 
-    def back_x(dx, dy):
-        which = 3 * (dx > 0) + dy + 1
-        return remote(
-            xsend.at[which], xrecv.at[which], bsend_sem, brecv_sem, slot_of(dx, dy, 0), (dx, 0, 0)
-        )
-
-    def back_y(dy):
-        which = 1 * (dy > 0)
-        return remote(
-            ysend.at[which], yrecv.at[which], bsend_sem, brecv_sem, slot_of(0, dy, 0), (0, dy, 0)
-        )
+    def back_z(dx, dy, dz, chunk):
+        lane = lane_z(dx, dy, dz)
+        return back(zsend, zrecv, lane, slot_of(dx, dy, dz), chunk, (0, 0, dz))
+
+    def back_x(dx, dy, chunk):
+        return back(xsend, xrecv, lane_x(dx, dy), slot_of(dx, dy, 0), chunk, (dx, 0, 0))
+
+    def back_y(dy, chunk):
+        return back(ysend, yrecv, 1 * (dy > 0), slot_of(0, dy, 0), chunk, (0, dy, 0))
 
     def back_place(axis, side):
         at = 1 * (side > 0)
@@ -505,14 +550,16 @@
             for part in range(2)
         ]
 
-    def send_pairs(row, columns):
-        rows = dot(drows[...], onehot[row : row + 128 * len(columns), :], NT)
-        for at, (dx, dy) in enumerate(columns):
-            blocks_ = folded(rows[:, 128 * at : 128 * at + 128])
-            for dz, value in zip((-1, 1), blocks_):
-                which = slot_of(dx, dy, dz) - (2 if (dx, dy) == (0, 0) else PAIR0 // SEND - 2)
-                zsend[which] = value.astype(BF16)
-                start(back_z(dx, dy, dz))
+    def send_pairs(rank):
+        row = PAIR0 + 128 * rank
+        rows = dot(drows[...], onehot[row : row + 256, :], NT)
+        for at in range(2):
+            for dz, value in zip((-1, 1), folded(rows[:, 128 * at : 128 * at + 128])):
+                zsend[lane_z(*ORDER[rank + at], dz)] = value.astype(BF16)
+        for chunk in range(CHUNKS):
+            for dx, dy in ORDER[rank : rank + 2]:
+                for dz in (-1, 1):
+                    start(back_z(dx, dy, dz, chunk))
 
     def keep_flats(rank):
         rows = dot(drows[...], onehot[FLAT0 + SEND * rank : FLAT0 + SEND * rank + 256, :], NT)
@@ -520,8 +567,46 @@
             for part, value in enumerate(folded(rows[:, 128 * at : 128 * at + 128])):
                 flat_g[rank + 2 * at + part] = value
 
-    for rank in (4, 6, 2):
-        send_pairs(PAIR0 + 128 * rank, ORDER[rank : rank + 2])
+    def arrived_z(dx, dy, chunk):
+        rows = slice(PIECE * chunk, PIECE * chunk + PIECE)
+        total = None
+        for dz in (-1, 1):
+            back_z(dx, dy, dz, chunk).wait_recv()
+            value = zrecv[lane_z(dx, dy, dz), rows, :].astype(F32)
+            total = value if total is None else total + value
+        if (dx, dy) == (0, 0):
+            return total
+        return total + flat_g[ORDER.index((dx, dy)), rows, :]
+
+    def arrived_x(dy, chunk):
+        rows = slice(PIECE * chunk, PIECE * chunk + PIECE)
+        total = arrived_z(0, dy, chunk)
+        for dx in (-1, 1):
+            back_x(dx, dy, chunk).wait_recv()
+            total = total + xrecv[lane_x(dx, dy), rows, :].astype(F32)
+        return total
+
+    def send_x(rank):
+        for chunk in range(CHUNKS):
+            rows = slice(PIECE * chunk, PIECE * chunk + PIECE)
+            for dx, dy in ORDER[rank : rank + 2]:
+                xsend[lane_x(dx, dy), rows, :] = arrived_z(dx, dy, chunk).astype(BF16)
+                start(back_x(dx, dy, chunk))
+
+    def send_y(chunk):
+        rows = slice(PIECE * chunk, PIECE * chunk + PIECE)
+        for dy in (-1, 1):
+            ysend[1 * (dy > 0), rows, :] = arrived_x(dy, chunk).astype(BF16)
+            start(back_y(dy, chunk))
+
+    send_pairs(4)
+    send_pairs(6)
+    keep_flats(4)
+    send_pairs(0)
+    keep_flats(0)
+    send_pairs(2)
+    send_x(4)
+    send_x(6)
 
     before = pre[...]
     sigmoid = 1.0 / (1.0 + jnp.exp(-before))
@@ -568,94 +653,93 @@
     for side in (-1, 1):
         start(back_place(2, side))
 
-    for rank in (4, 0):
-        keep_flats(rank)
-    send_pairs(PAIR0, ORDER[0:2])
-
-    def arrived_z(dx, dy):
-        total = None
-        for dz in (-1, 1):
-            back_z(dx, dy, dz).wait_recv()
-            which = slot_of(dx, dy, dz) - (2 if (dx, dy) == (0, 0) else PAIR0 // SEND - 2)
-            value = zrecv[which].astype(F32)
-            total = value if total is None else total + value
-        if (dx, dy) == (0, 0):
-            return total
-        return total + flat_g[ORDER.index((dx, dy))]
-
-    for dx, dy in (ORDER[4:] + ORDER[2:4]):
-        xsend[3 * (dx > 0) + dy + 1] = arrived_z(dx, dy).astype(BF16)
-        start(back_x(dx, dy))
+    send_x(2)
+    rows = dot(drows[...], onehot[0:FLAT0, :], NT)
+    own_g[...] = rows[:, 0:ATOMS] + dot(dlow[...], onehot[0:ATOMS, :], NT)
+    for dz, value in zip((-1, 1), folded(rows[:, ATOMS:FLAT0])):
+        zsend[lane_z(0, 0, dz)] = value.astype(BF16)
+        for chunk in range(CHUNKS):
+            start(back_z(0, 0, dz, chunk))
+
+    for chunk in range(CHUNKS - 1):
+        send_y(chunk)
     for side in (-1, 1):
         back_place(2, side).wait_recv()
     for side in (-1, 1):
         lines = pl.ds(3 + 3 * side, 3)
         pxsend[1 * (side > 0)] = pgrad[0, lines] + pzrecv[0, lines] + pzrecv[1, lines]
         start(back_place(0, side))
-
-    rows = dot(drows[...], onehot[0:FLAT0, :], NT)
-    own_g[...] = rows[:, 0:ATOMS] + dot(dlow[...], onehot[0:ATOMS, :], NT)
-    for dz, value in zip((-1, 1), folded(rows[:, ATOMS:FLAT0])):
-        zsend[1 * (dz > 0)] = value.astype(BF16)
-        start(back_z(0, 0, dz))
-
-    for dy in (-1, 1, 0):
-        total = arrived_z(0, dy)
-        for dx in (-1, 1):
-            back_x(dx, dy).wait_recv()
-            total = total + xrecv[3 * (dx > 0) + dy + 1].astype(F32)
-        if dy:
-            ysend[1 * (dy > 0)] = total.astype(BF16)
-            start(back_y(dy))
-        if dy == 1:
-            for side in (-1, 1):
-                back_place(0, side).wait_recv()
-            middle = pl.ds(3, 3)
-            totals = pgrad[0, middle]
-            totals = totals + pzrecv[0, middle] + pzrecv[1, middle] + pxrecv[0] + pxrecv[1]
-            pysend[0] = totals[0]
-            pysend[1] = totals[2]
-            for side in (-1, 1):
-                start(back_place(1, side))
-    for dy in (-1, 1):
-        back_y(dy).wait_recv()
-        total = total + yrecv[1 * (dy > 0)].astype(F32)
-    high, rest = split(total)
-    for part, chosen in enumerate((picks_left, picks_right)):
-        rows = slice(HALF * part, HALF * part + HALF)
-        own_g[rows, :] += dot(high, chosen, NT) + dot(rest, chosen, NT)
-    for tile in range(4):
-        rows = slice(128 * tile, 128 * tile + 128)
-        high, rest = split(own_g[rows, :])
-        fgrad_ref[rows, :] = dot(mix[tile], high) + dot(mix[tile], rest)
-    high, rest = split(own_g[512:FEAT, :])
-    fgrad_ref[512:FEAT, :] = dot(mix_ref[2], high) + dot(mix_ref[2], rest)
-
-    back = totals[1]
+    send_y(CHUNKS - 1)
+    for side in (-1, 1):
+        back_place(0, side).wait_recv()
+    middle = pl.ds(3, 3)
+    totals = pgrad[0, middle] + pzrecv[0, middle] + pzrecv[1, middle] + pxrecv[0] + pxrecv[1]
+    pysend[0] = totals[0]
+    pysend[1] = totals[2]
+    for side in (-1, 1):
+        start(back_place(1, side))
+    for chunk in range(CHUNKS):
+        total = arrived_x(0, chunk)
+        for dy in (-1, 1):
+            back_y(dy, chunk).wait_recv()
+            total = total + yrecv[1 * (dy > 0), PIECE * chunk : PIECE * chunk + PIECE, :].astype(F32)
+        high, rest = split(total)
+        for part, chosen in enumerate((picks_left, picks_right)):
+            at = HALF * part + PIECE * chunk
+            owned_ref[at : at + PIECE, :] = (
+                own_g[at : at + PIECE, :] + dot(high, chosen, NT) + dot(rest, chosen, NT)
+            )
+
+    final = totals[1]
     for side in (-1, 1):
         back_place(1, side).wait_recv()
-        back = back + pyrecv[1 * (side > 0)]
-    force = moved - own_place[0:3] - joined(dot(parts(back).astype(BF16), picks_left, NT))[0:3]
+        final = final + pyrecv[1 * (side > 0)]
+    force = moved - own_place[0:3] - joined(dot(parts(final).astype(BF16), picks_left, NT))[0:3]
     for axis in range(3):
         force_ref[axis] = force[axis : axis + 1]
     for copy in started:
         copy.wait_send()
 
 
+def finish(energy_in, force_in, owned_in, mix_ref, energy_ref, force_ref, fgrad_ref):
+    energy_ref[...] = energy_in[...]
+    force_ref[...] = force_in[...]
+    mix = mixers(mix_ref)
+    for tile in range(4):
+        rows = slice(128 * tile, 128 * tile + 128)
+        high, rest = split(owned_in[rows, :])
+        fgrad_ref[rows, :] = dot(mix[tile], high) + dot(mix[tile], rest)
+    high, rest = split(owned_in[512:FEAT, :])
+    fgrad_ref[512:FEAT, :] = dot(mix_ref[2], high) + dot(mix_ref[2], rest)
+
+
 def shards(
     positions, features, species, neighbours, send_list, mix_weight, radial_in, radial_out, readout
 ):
     vmem = pl.BlockSpec(memory_space=pltpu.VMEM)
-    energy, forces, feature_grad = pl.pallas_call(
+    results = (
+        jax.ShapeDtypeStruct((1, ATOMS), F32),
+        jax.ShapeDtypeStruct((3, 1, ATOMS), F32),
+        jax.ShapeDtypeStruct((FEAT, ATOMS), F32),
+    )
+    arguments = (
+        positions.reshape(3, 1, ATOMS),
+        features[0, 0, 0].T,
+        species[0, 0],
+        neighbours.reshape(SLOTS, 1, ATOMS),
+        send_list[0, 0],
+        mix_weight,
+        radial_in,
+        radial_out,
+        jnp.transpose(readout, (1, 0, 2)),
+    )
+    energy, forces, owned = pl.pallas_call(
         kernel,
-        out_shape=(
-            jax.ShapeDtypeStruct((1, ATOMS), F32),
-            jax.ShapeDtypeStruct((3, 1, ATOMS), F32),
-            jax.ShapeDtypeStruct((FEAT, ATOMS), F32),
-        ),
-        in_specs=[vmem] * 9,
+        out_shape=results,
+        in_specs=[pl.BlockSpec(memory_space=pltpu.HBM)] * 9,
         out_specs=(vmem, vmem, vmem),
-        scratch_shapes=[
+        scratch_shapes=[pltpu.VMEM(each.shape, each.dtype) for each in arguments]
+        + [
             pltpu.VMEM((HALF, 128), BF16),
             pltpu.VMEM((BLOCKS, HALF, 128), BF16),
             pltpu.VMEM((3, 9, 8, 128), F32),
@@ -693,28 +777,27 @@
             pltpu.VMEM((2, 3, 8, 128), F32),
             pltpu.VMEM((2, 8, 128), F32),
             pltpu.VMEM((2, 8, 128), F32),
-            pltpu.SemaphoreType.DMA((BLOCKS,)),
-            pltpu.SemaphoreType.DMA((BLOCKS,)),
-            pltpu.SemaphoreType.DMA((BLOCKS,)),
-            pltpu.SemaphoreType.DMA((BLOCKS,)),
+            pltpu.SemaphoreType.DMA((CHUNKS * BLOCKS,)),
+            pltpu.SemaphoreType.DMA((CHUNKS * BLOCKS,)),
+            pltpu.SemaphoreType.DMA((CHUNKS * BLOCKS,)),
+            pltpu.SemaphoreType.DMA((CHUNKS * BLOCKS,)),
             pltpu.SemaphoreType.DMA((12,)),
             pltpu.SemaphoreType.DMA((12,)),
+            pltpu.SemaphoreType.DMA((9,)),
         ],
         compiler_params=pltpu.CompilerParams(
-            collective_id=0, has_side_effects=True, vmem_limit_bytes=60 * 1024 * 1024
+            collective_id=0, has_side_effects=True, vmem_limit_bytes=40 * 1024 * 1024
         ),
         name="layer",
-    )(
-        positions.reshape(3, 1, ATOMS),
-        features[0, 0, 0].T,
-        species[0, 0],
-        neighbours.reshape(SLOTS, 1, ATOMS),
-        send_list[0, 0],
-        mix_weight,
-        radial_in,
-        radial_out,
-        jnp.transpose(readout, (1, 0, 2)),
-    )
+    )(*[pltpu.with_memory_space_constraint(each, pltpu.HBM) for each in arguments])
+    energy, forces, feature_grad = pl.pallas_call(
+        finish,
+        out_shape=results,
+        in_specs=[vmem] * 4,
+        out_specs=(vmem, vmem, vmem),
+        compiler_params=pltpu.CompilerParams(vmem_limit_bytes=4 * 1024 * 1024),
+        name="finish",
+    )(energy, forces, owned, mix_weight)
     return (
         energy[None, None],
         forces.reshape(1, 1, 1, 3, ATOMS),

time: 75.3 us -> 73.8 us (0.980)
  local copies, waits for them, and re-layouts: 3.36 us -> 0.01 us
  Pallas kernels: 71.1 us -> 72.3 us
    unnamed x7 -> x2, local copies, waits for them, and re-layouts: 3.36 us -> 0.01 us
    pallas_call x1 -> x2, Pallas kernels: 71.1 us -> 72.3 us  [the longest x1 71.3 us: shards(): pl.pallas_call(kernel, out_shape=results, in_specs=[pl.BlockSpec(memory_s...]
where the time goes in v3:
time: 73.8 us; the launch traced here: 72.9 us
  Pallas kernels  72.3 us (98%)
    pallas_call x1, Pallas kernels, shards(): pl.pallas_call(kernel, out_shape=results, in_specs=[pl.BlockSpec(memory_s...  71.3 us

profile of v3, /device:TPU:6, one launch (start us, length us, event | category | flops | bytes accessed | tf_op | source)
XLA Modules:
  0.0 72.9 jit_solution(17025500457482466466)
XLA Ops:
  0.6 0.0 copy-start
  0.6 71.3 %layer.1 = (f32[1,128]{1,0:T(1,128)S(1)}, f32[3,1,128]{2,1,0:T(1,128)S(1)}, f32[576,128]{1,0:T(8,128)S(1)}) custom-call(f32[3,1,128]{2,1,0:T(1,128)} %bitcast.18, bf16[576,128]{1,0:T(8,128)(2,1)} %bitcast.15, s32[1,128]{1,0:T(1,128)} %bitcast.19, s32[12,1,128]{2,1,0:T(1,128)} %bitcast.16, s32[1,64]{1,0:T(1,128)} %bitcast.20, bf16[3,64,64]{2,1,0:T(8,128)(2,1)} %mix_ref.1, ...), custom_call_target="tpu_custom_call" | custom-call | tf_op jit(solution)/shard_map/layer/pallas_call | solution.py:736
  71.9 0.0 copy-done
  71.9 1.0 %finish.1 = (f32[1,128]{1,0:T(1,128)}, f32[3,1,128]{2,1,0:T(1,128)}, f32[576,128]{1,0:T(8,128)}) custom-call(f32[1,128]{1,0:T(1,128)S(1)} %get-tuple-element.9.energy_in, f32[3,1,128]{2,1,0:T(1,128)S(1)} %get-tuple-element.10.force_in, f32[576,128]{1,0:T(8,128)S(1)} %get-tuple-element.11.owned_in, bf16[3,64,64]{2,1,0:T(8,128)(2,1)S(1)} %copy-done), custom_call_target="tpu_custom_call" | custom-call | tf_op jit(solution)/shard_map/finish/pallas_call | solution.py:793
Async XLA Ops:
  0.6 71.3 %copy-start = (bf16[3,64,64]{2,1,0:T(8,128)(2,1)S(1)}, bf16[3,64,64]{2,1,0:T(8,128)(2,1)}, u32[]{:S(2)}) copy-start(bf16[3,64,64]{2,1,0:T(8,128)(2,1)} %mix_ref.1) | copy-start | bytes 73732

commit v4 on v3

--- a/solution.py
+++ b/solution.py
@@ -22,7 +22,7 @@
 CH = 64
 FEAT = 576
 HALF = 288
-CHUNKS = 3
+CHUNKS = 2
 PIECE = HALF // CHUNKS
 RUN = 4
 
@@ -206,6 +206,11 @@
         copy.start()
         started.append(copy)
 
+    def drain():
+        for copy in started:
+            copy.wait_send()
+        started.clear()
+
     def remote(source, target, sends, recvs, which, go):
         return pltpu.make_async_remote_copy(
             src_ref=source,
@@ -247,12 +252,8 @@
 
     for side in (-1, 1):
         start(halo_place(1, side))
-    for chunk in range(CHUNKS):
-        for dy in (-1, 1):
-            start(halo(0, dy, 0, 1, chunk))
-    for chunk in range(CHUNKS):
-        for dx in (-1, 1):
-            start(halo(dx, 0, 0, 0, chunk))
+    for dy in (-1, 1):
+        start(halo(0, dy, 0, 1, 0))
     for chunk in range(CHUNKS):
         for dz in (-1, 1):
             start(halo(0, 0, dz, 2, chunk))
@@ -328,10 +329,6 @@
 
         lax.fori_loop(0, EDGES // 256, one, 0)
 
-    for side in (-1, 1):
-        halo_place(1, side).wait_recv()
-    for side in (-1, 1):
-        start(halo_place(0, side))
     def pass_x(dy, chunk):
         halo(0, dy, 0, 1, chunk).wait_recv()
         for dx in (-1, 1):
@@ -344,29 +341,37 @@
         for dz in (-1, 1):
             start(halo(dx, dy, dz, 2, chunk))
 
+    drain()
+    for chunk in range(1, CHUNKS):
+        for dy in (-1, 1):
+            start(halo(0, dy, 0, 1, chunk))
+        for dz in (-1, 1):
+            halo(0, 0, dz, 2, chunk - 1).wait_recv()
+        if chunk == CHUNKS - 1:
+            for dz in (-1, 1):
+                halo(0, 0, dz, 2, chunk).wait_recv()
+            settle_pair(0, 0)
+            gather(0, FLAT0)
+        drain()
+    for side in (-1, 1):
+        halo_place(1, side).wait_recv()
+    for side in (-1, 1):
+        start(halo_place(0, side))
     for chunk in range(CHUNKS):
+        for dx in (-1, 1):
+            start(halo(dx, 0, 0, 0, chunk))
+    for dy in (-1, 1):
+        pass_x(dy, 0)
+    for side in (-1, 1):
+        halo_place(0, side).wait_recv()
+    for side in (-1, 1):
+        start(halo_place(2, side))
+    for chunk in range(1, CHUNKS):
         for dy in (-1, 1):
             pass_x(dy, chunk)
-    for side in (-1, 1):
-        halo_place(0, side).wait_recv()
-    for side in (-1, 1):
-        start(halo_place(2, side))
     for chunk in range(CHUNKS):
         for dx in (-1, 1):
             pass_z(dx, 0, chunk)
-    for dz in (-1, 1):
-        wait_halo(0, 0, dz, 2)
-    settle_pair(0, 0)
-    gather(0, FLAT0)
-    for chunk in range(CHUNKS):
-        for dy in (-1, 1):
-            for dx in (-1, 1):
-                pass_z(dx, dy, chunk)
-    for rank in range(0, 8, 2):
-        left = FLAT0 // SEND + rank
-        settle(SEND * left, left, left + 1)
-    gather(FLAT0, PAIR0)
-
     for side in (-1, 1):
         halo_place(2, side).wait_recv()
     for half in range(2):
@@ -416,6 +421,15 @@
     pre[...] = before
     hidden = before / (1.0 + jnp.exp(-before))
     radial[...] = dot(rout_ref[...], hidden, TN, HIGH)
+
+    for chunk in range(CHUNKS):
+        for dy in (-1, 1):
+            for dx in (-1, 1):
+                pass_z(dx, dy, chunk)
+    for rank in range(0, 8, 2):
+        left = FLAT0 // SEND + rank
+        settle(SEND * left, left, left + 1)
+    gather(FLAT0, PAIR0)
 
     for dx, dy in ORDER[:4]:
         for dz in (-1, 1):
@@ -550,12 +564,14 @@
             for part in range(2)
         ]
 
-    def send_pairs(rank):
+    def make_pairs(rank):
         row = PAIR0 + 128 * rank
         rows = dot(drows[...], onehot[row : row + 256, :], NT)
         for at in range(2):
             for dz, value in zip((-1, 1), folded(rows[:, 128 * at : 128 * at + 128])):
                 zsend[lane_z(*ORDER[rank + at], dz)] = value.astype(BF16)
+
+    def start_pairs(rank):
         for chunk in range(CHUNKS):
             for dx, dy in ORDER[rank : rank + 2]:
                 for dz in (-1, 1):
@@ -599,12 +615,18 @@
             ysend[1 * (dy > 0), rows, :] = arrived_x(dy, chunk).astype(BF16)
             start(back_y(dy, chunk))
 
-    send_pairs(4)
-    send_pairs(6)
+    drain()
+    make_pairs(4)
+    start_pairs(4)
+    make_pairs(6)
+    start_pairs(6)
     keep_flats(4)
-    send_pairs(0)
+    make_pairs(0)
     keep_flats(0)
-    send_pairs(2)
+    make_pairs(2)
+    drain()
+    start_pairs(0)
+    start_pairs(2)
     send_x(4)
     send_x(6)
 
@@ -653,7 +675,6 @@
     for side in (-1, 1):
         start(back_place(2, side))
 
-    send_x(2)
     rows = dot(drows[...], onehot[0:FLAT0, :], NT)
     own_g[...] = rows[:, 0:ATOMS] + dot(dlow[...], onehot[0:ATOMS, :], NT)
     for dz, value in zip((-1, 1), folded(rows[:, ATOMS:FLAT0])):
@@ -663,6 +684,8 @@
 
     for chunk in range(CHUNKS - 1):
         send_y(chunk)
+    if CHUNKS == 1:
+        send_x(2)
     for side in (-1, 1):
         back_place(2, side).wait_recv()
     for side in (-1, 1):
@@ -670,6 +693,8 @@
         pxsend[1 * (side > 0)] = pgrad[0, lines] + pzrecv[0, lines] + pzrecv[1, lines]
         start(back_place(0, side))
     send_y(CHUNKS - 1)
+    if CHUNKS > 1:
+        send_x(2)
     for side in (-1, 1):
         back_place(0, side).wait_recv()
     middle = pl.ds(3, 3)

time: 73.8 us -> 75.1 us (1.018)
  Pallas kernels: 72.3 us -> 74.2 us
    pallas_call x1, Pallas kernels: 71.3 us -> 73.2 us  [shards(): pl.pallas_call(kernel, out_shape=results, in_specs=[pl.BlockSpec(memory_s...]
where the time goes in v4:
time: 75.1 us; the launch traced here: 74.9 us
  Pallas kernels  74.2 us (99%)
    pallas_call x1, Pallas kernels, shards(): pl.pallas_call(kernel, out_shape=results, in_specs=[pl.BlockSpec(memory_s...  73.2 us

profile of v4, /device:TPU:6, one launch (start us, length us, event | category | flops | bytes accessed | tf_op | source)
XLA Modules:
  0.0 74.9 jit_solution(13567332437478224074)
XLA Ops:
  0.6 0.0 copy-start
  0.6 73.2 %layer.1 = (f32[1,128]{1,0:T(1,128)S(1)}, f32[3,1,128]{2,1,0:T(1,128)S(1)}, f32[576,128]{1,0:T(8,128)S(1)}) custom-call(f32[3,1,128]{2,1,0:T(1,128)} %bitcast.18, bf16[576,128]{1,0:T(8,128)(2,1)} %bitcast.15, s32[1,128]{1,0:T(1,128)} %bitcast.19, s32[12,1,128]{2,1,0:T(1,128)} %bitcast.16, s32[1,64]{1,0:T(1,128)} %bitcast.20, bf16[3,64,64]{2,1,0:T(8,128)(2,1)} %mix_ref.1, ...), custom_call_target="tpu_custom_call" | custom-call | tf_op jit(solution)/shard_map/layer/pallas_call | solution.py:761
  73.9 0.0 copy-done
  73.9 1.0 %finish.1 = (f32[1,128]{1,0:T(1,128)}, f32[3,1,128]{2,1,0:T(1,128)}, f32[576,128]{1,0:T(8,128)}) custom-call(f32[1,128]{1,0:T(1,128)S(1)} %get-tuple-element.9.energy_in, f32[3,1,128]{2,1,0:T(1,128)S(1)} %get-tuple-element.10.force_in, f32[576,128]{1,0:T(8,128)S(1)} %get-tuple-element.11.owned_in, bf16[3,64,64]{2,1,0:T(8,128)(2,1)S(1)} %copy-done), custom_call_target="tpu_custom_call" | custom-call | tf_op jit(solution)/shard_map/finish/pallas_call | solution.py:818
Async XLA Ops:
  0.6 73.2 %copy-start = (bf16[3,64,64]{2,1,0:T(8,128)(2,1)S(1)}, bf16[3,64,64]{2,1,0:T(8,128)(2,1)}, u32[]{:S(2)}) copy-start(bf16[3,64,64]{2,1,0:T(8,128)(2,1)} %mix_ref.1) | copy-start | bytes 73732
